TPU v7x, 256 devices: a whole 4x4x8 slice. The times are simulated.
256 devices in a mesh: rows: 64 (over z, x, core), grp: 4 (over y).
Axes of the slice: x: 4, y: 4, z: 8, core: 2. Of those that a mesh axis runs over, the one named last changes fastest.
Arguments:
- user_features: bfloat16 [4, 16384, 256], P('grp', 'rows'), may hold values from -72 to 72
- w_first: bfloat16 [256, 256], replicated, may hold values from -0.375 to 0.375
- w_second: bfloat16 [256, 256], replicated, may hold values from -0.375 to 0.375
- item_embed: bfloat16 [4, 16384, 256], P('grp', 'rows'), may hold values from -27 to 27
- example_weight: float32 [4, 16384], P('grp', 'rows'), may hold values from 0.02 to 0.2
- positive: int32 [4, 16384], P('grp', 'rows'), may hold values from 0 to 16383
- item_owner: int32 [4, 16384, 1], P('grp', 'rows'), may hold values from 0 to 63; in each aligned block of 256 rows (0 to 255, 256 to 511, ..., all dimensions but the last counted through in order) at most 16 rows name the same one
- item_row: int32 [4, 16384], P('grp', 'rows'), may hold values from 0 to 4095
Outputs:
- grad_first: float32 [256, 256], replicated
- grad_second: float32 [256, 256], replicated
- grad_table: float32 [262144, 256], P('rows', 'grp')
Inputs may be any that keep to these rules, and one draw needn't show every extreme that they name: `item_owner`: within the rows of one device (aligned blocks of 256 pairs of a group) no owner is named by more than 16 pairs, a bound that some block reaches.
All inputs are finite; a program needn't handle non-finite values.
Results may differ from a plain program's by a relative error of at most 0.0023.
The roundings to bfloat16 on the way count: a program that leaves them out, or rounds other values in their place, can miss the bound.
Values may be sent and summed in bfloat16 or wider, within the bound.
No kernel may reach another device: no remote copies, remote signals or barrier semaphores. Data moves between devices by JAX's collectives and lax.ppermute only.
A program may use at most 128 MiB of HBM per device.

v0:
```python
import jax
import jax.numpy as jnp
from jax import lax
from jax.experimental import pallas as pl
from jax.experimental.pallas import tpu as pltpu
from jax.sharding import Mesh
from jax.sharding import PartitionSpec as P

TABLE = 4096
CAP = 16
BLK = 256
ROWS = 8 * BLK
XK = ("x", "k")
KYX = ("k", "y", "x")
YZXK = ("y", "z", "x", "k")
F32 = jnp.float32
BF16 = jnp.bfloat16
VMEM = pl.BlockSpec(memory_space=pltpu.VMEM)
SMEM = pl.BlockSpec(memory_space=pltpu.SMEM)


def dot(left, right, dims):
    return lax.dot_general(left, right, ((dims[0:1], dims[1:2]), ((), ())), preferred_element_type=F32)


def exchange(value, axes):
    return lax.all_to_all(value, axes, 0, 0, tiled=True)


def to_all(value, axes):
    return exchange(jnp.broadcast_to(value[None], (lax.axis_size(axes), *value.shape)), axes)


def shifted(value, axis, step):
    count = lax.axis_size(axis)
    return lax.ppermute(value, axis, [(i, (i + step) % count) for i in range(count)])


def place(axis, step=0):
    return (lax.axis_index(axis).astype(jnp.uint32) + jnp.uint32(step)) & jnp.uint32(lax.axis_size(axis) - 1)


def rows_at(value, start, count):
    zero = jnp.uint32(0)
    return lax.dynamic_slice(value, (start,) + (zero,) * (value.ndim - 1), (count, *value.shape[1:]))


def summed_share(value, axis):
    count = lax.axis_size(axis)
    rows = value.shape[0] // count
    total = rows_at(value, place(axis) * jnp.uint32(rows), rows)
    for d in range(1, count):
        total = total + shifted(rows_at(value, place(axis, d) * jnp.uint32(rows), rows), axis, d)
    return total


def joined(value, axis):
    count = lax.axis_size(axis)
    tiles = [value] + [shifted(value, axis, d) for d in range(1, count)]
    rising = [tiles[-d % count] for d in range(count)]
    rows = value.shape[0]
    start = (jnp.uint32(count) - place(axis)) * jnp.uint32(rows)
    return rows_at(jnp.concatenate(rising + rising, axis=0), start, count * rows)


def stats_kernel(at_ref, items_ref, users_ref, own_ref, out_ref):
    for b in range(8):
        scores = dot(items_ref[...], users_ref[b * BLK : (b + 1) * BLK, :], (1, 1))
        top = jnp.max(scores, axis=0, keepdims=True)
        out_ref[0, pl.ds(at_ref[b], 1), :] = top
        out_ref[0, pl.ds(8 + at_ref[b], 1), :] = jnp.sum(jnp.exp(scores - top), axis=0, keepdims=True)
    out_ref[0, 16:40, :] = own_ref[...]
    for p in range(1, 8):
        out_ref[p] = out_ref[0]


def stats(at, items, users, own):
    return pl.pallas_call(
        stats_kernel,
        in_specs=[SMEM, VMEM, VMEM, VMEM],
        out_shape=jax.ShapeDtypeStruct((8, 40, BLK), F32),
        compiler_params=pltpu.CompilerParams(vmem_limit_bytes=20 * 2**20),
        name="stats",
    )(at, items, users, own)


def users_kernel(
    at_ref, items_ref, users_ref, got_ref, all_ref, keep_ref, give_ref, turned_ref, index_ref
):
    turned_ref[...] = items_ref[...].T
    spot = lax.broadcasted_iota(jnp.int32, (ROWS, BLK), 0)
    index_ref[...] = (spot // BLK) * ROWS + spot % BLK + at_ref[8]
    for b in range(8):
        c = at_ref[b]
        tops = got_ref[:, pl.ds(c, 1), :].reshape(8, BLK)
        parts = got_ref[:, pl.ds(8 + c, 1), :].reshape(8, BLK)
        own = got_ref[pl.ds(c, 1), 16:18, :].reshape(2, BLK)
        weight = own[0:1]
        target = own[1:2].astype(jnp.int32)
        top = jnp.max(tops, axis=0, keepdims=True)
        total = top + jnp.log(jnp.sum(parts * jnp.exp(tops - top), axis=0, keepdims=True))
        total = total - jnp.log(weight)
        scores = dot(items_ref[...], users_ref[b * BLK : (b + 1) * BLK, :], (1, 1))
        share = jnp.exp(scores - total)
        dscore = jnp.where(index_ref[...] == target, share - weight, share).astype(BF16)
        all_ref[:, b * BLK : (b + 1) * BLK] = dscore
        part = dot(turned_ref[...], dscore, (1, 0))
        if b % 2 == 0:
            keep_ref[b // 2] = part
        else:
            give_ref[b // 2] = part


def user_side(at, items, users, got):
    share = jax.ShapeDtypeStruct((4, 256, BLK), F32)
    return pl.pallas_call(
        users_kernel,
        in_specs=[SMEM, VMEM, VMEM, VMEM],
        out_specs=[VMEM] * 3,
        out_shape=[jax.ShapeDtypeStruct((ROWS, ROWS), BF16), share, share],
        scratch_shapes=[pltpu.VMEM((256, ROWS), BF16), pltpu.VMEM((ROWS, BLK), jnp.int32)],
        compiler_params=pltpu.CompilerParams(vmem_limit_bytes=32 * 2**20),
        name="user_side",
    )(at, items, users, got)


def items_kernel(at_ref, all_ref, users_ref, got_ref, gi_ref, ids_ref):
    largest = jnp.max(jnp.abs(users_ref[...].astype(F32)), axis=0, keepdims=True)
    largest = jnp.maximum(jnp.max(largest, axis=1, keepdims=True) * 416.0, 1e-30)
    power = jnp.ceil(jnp.log(largest) * 1.4426950408889634)
    gi = dot(all_ref[...], users_ref[...], (1, 0)) * jnp.exp2(15.0 - power)
    for z in range(8):
        gi_ref[z, :BLK, :] = gi[z * BLK : (z + 1) * BLK]
    lane = lax.broadcasted_iota(jnp.int32, (8, 128), 1) // CAP
    ids_ref[...] = jnp.zeros_like(ids_ref)
    for y in range(4):
        row = jnp.zeros((8, 128), F32)
        for p in range(8):
            piece = got_ref[p, 24 + 8 * (y // 2) : 32 + 8 * (y // 2), 128 * (y % 2) : 128 * (y % 2) + 128]
            turn = ((p - at_ref[9]) & 7) * CAP
            row = jnp.where(lane == p, pltpu.roll(piece, turn, 1), row)
        high = jnp.floor(row * (1.0 / 64.0))
        ids_ref[:, y, :128] = high
        ids_ref[:, y, 128:] = row - 64.0 * high
    ids_ref[:, 4, :] = jnp.broadcast_to(power, (8, 256))
    gi_ref[:, BLK:, :] = ids_ref[...]


def item_side(at, dscore, users, got):
    return pl.pallas_call(
        items_kernel,
        in_specs=[SMEM, VMEM, VMEM, VMEM],
        out_specs=VMEM,
        out_shape=jax.ShapeDtypeStruct((8, BLK + 8, 256), F32),
        scratch_shapes=[pltpu.VMEM((8, 8, 256), F32)],
        compiler_params=pltpu.CompilerParams(vmem_limit_bytes=22 * 2**20),
        name="item_side",
    )(at, dscore, users, got)


def tower_kernel(
    core_ref, own_ref, one_ref, two_ref, three_ref, features_ref, first_ref, second_ref,
    keep_ref, give_ref,
):
    grad_user = (own_ref[0] + one_ref[...] + two_ref[...] + three_ref[...]).astype(BF16)
    features = features_ref[...].T
    pre_act = dot(first_ref[...].T, features, (1, 0))
    hidden = jax.nn.silu(pre_act).astype(BF16)
    d_second = dot(hidden, grad_user, (1, 1))
    back_grad = dot(second_ref[...], grad_user, (1, 0))
    gate = jax.nn.sigmoid(pre_act)
    grad_pre = (back_grad * gate * (1.0 + pre_act * (1.0 - gate))).astype(BF16)
    d_first = dot(features, grad_pre, (1, 1))

    @pl.when(core_ref[0] == 0)
    def _():
        keep_ref[...] = d_first
        give_ref[...] = d_second

    @pl.when(core_ref[0] != 0)
    def _():
        keep_ref[...] = d_second
        give_ref[...] = d_first


def tower_grads(core, parts, features, w_first, w_second):
    return pl.pallas_call(
        tower_kernel,
        in_specs=[SMEM] + [VMEM] * 7,
        out_specs=[VMEM] * 2,
        out_shape=[jax.ShapeDtypeStruct((256, 256), F32)] * 2,
        compiler_params=pltpu.CompilerParams(vmem_limit_bytes=16 * 2**20),
        name="tower_grads",
    )(core, *parts, features, w_first, w_second)


def pack_kernel(item_ref, owner_ref, rank_ref, out_ref):
    lane = lax.broadcasted_iota(jnp.int32, (64 * 8, BLK), 0)
    halves = []
    for h in range(2):
        rank = rank_ref[...] - 8 * h
        slot = jnp.where((rank >= 0) & (rank < 8), owner_ref[...] * 8 + rank, -1)
        pick = (lane == slot).astype(F32).astype(BF16)
        halves.append(dot(pick, item_ref[...], (1, 0)))
    for g in range(4):
        share = slice(64 * g, 64 * g + 64)
        both = jnp.concatenate([halves[0][:, share], halves[1][:, share]], axis=1)
        out_ref[g * 512 : (g + 1) * 512, :] = both.astype(BF16)


def pack(item, owner, rank):
    return pl.pallas_call(
        pack_kernel,
        in_specs=[VMEM] * 3,
        out_shape=jax.ShapeDtypeStruct((4 * 512, 128), BF16),
        compiler_params=pltpu.CompilerParams(vmem_limit_bytes=16 * 2**20),
        name="pack",
    )(item, owner, rank)


def table_kernel(got_ref, ids_ref, out_ref, pick_ref, kept_ref):
    both = got_ref[...].T
    value = jnp.concatenate([both[:64], both[64:]], axis=1)
    ids = ids_ref[...]
    upper = ids >> 8
    lower = ids & 255
    pick = (lax.broadcasted_iota(jnp.int32, (256, TABLE), 0) == lower).astype(F32).astype(BF16)
    pick_ref[...] = pick.T

    def step(j, carry):
        for q in range(4):
            keep = jnp.broadcast_to((upper == 4 * j + q).astype(F32), (16, TABLE)).astype(BF16)
            kept_ref[q * 64 : (q + 1) * 64, :] = value * jnp.concatenate([keep] * 4, axis=0)
        part = dot(kept_ref[...], pick_ref[...], (1, 0))
        for q in range(4):
            at = pl.multiple_of((4 * j + q) * 256, 256)
            out_ref[:, pl.ds(at, 256)] = part[q * 64 : (q + 1) * 64]
        return carry

    lax.fori_loop(0, 4, step, 0)


def table(got, ids):
    return pl.pallas_call(
        table_kernel,
        in_specs=[VMEM] * 2,
        out_shape=jax.ShapeDtypeStruct((64, TABLE), F32),
        scratch_shapes=[pltpu.VMEM((TABLE, 256), BF16), pltpu.VMEM((256, TABLE), BF16)],
        compiler_params=pltpu.CompilerParams(vmem_limit_bytes=28 * 2**20),
        name="table",
    )(got, ids)


def tower(features, w_first, w_second):
    pre_act = jnp.dot(features, w_first, preferred_element_type=F32)
    hidden = jax.nn.silu(pre_act).astype(BF16)
    return pre_act, hidden, jnp.dot(hidden, w_second, preferred_element_type=F32).astype(BF16)


def step_body(
    user_features, w_first, w_second, item_embed, example_weight, positive, item_owner, item_row
):
    features = user_features[0]
    owner = item_owner.reshape(1, BLK)
    items = to_all(item_embed[0], "z").reshape(ROWS, 256)
    pair = jnp.concatenate([features, shifted(features, "k", 1)], axis=0)
    block = jnp.concatenate([pair] + [shifted(pair, "x", d) for d in range(1, 4)], axis=0)
    _, _, users = tower(block, w_first, w_second)
    block_no = jnp.arange(8, dtype=jnp.int32)
    source = 2 * ((lax.axis_index("x") - block_no // 2) & 3) + ((block_no % 2) ^ lax.axis_index("k"))
    own_place = lax.axis_index(XK).reshape(1)
    at = jnp.concatenate([source, own_place * BLK, own_place]).astype(jnp.int32)

    member = (owner == lax.broadcasted_iota(jnp.int32, (64, 1), 0)).astype(F32)
    order = lax.broadcasted_iota(jnp.int32, (BLK, BLK), 0) < lax.broadcasted_iota(jnp.int32, (BLK, BLK), 1)
    before = dot(member.astype(BF16), order.astype(BF16), (1, 0))
    rank = jnp.sum(before * member, axis=0, keepdims=True).astype(jnp.int32)
    slot = owner * CAP + rank
    held = (slot == lax.broadcasted_iota(jnp.int32, (64 * CAP, 1), 0)).astype(jnp.int32)
    rows = jnp.sum(held * (item_row + 1), axis=1).astype(F32).reshape(64, CAP)
    rows = joined(rows, "y")
    rows = rows.reshape(2, 2, 8, 128).swapaxes(1, 2).reshape(16, BLK)
    own = jnp.concatenate(
        [example_weight, positive.astype(F32), jnp.zeros((6, BLK), F32), rows], axis=0
    )
    got = exchange(stats(at, items, users, own), XK)
    dscore, keep, give = user_side(at, items, users, got)
    swapped = shifted(give, "k", 1)
    gi = item_side(at, dscore, users, got)
    gi = exchange(gi.astype(jnp.float16), "z")
    gu = keep + swapped
    parts = [gu] + [shifted(gu[d], "x", -d) for d in range(1, 4)]
    scale = jnp.exp2(gi[:, BLK + 4, 0].astype(F32) - 15.0)
    item = sum(gi[z, :BLK].astype(F32) * scale[z] for z in range(8)).astype(BF16)
    ids = gi[:, BLK : BLK + 4, :].astype(F32)
    ids = (64.0 * ids[:, :, :128] + ids[:, :, 128:]).astype(jnp.int32) - 1
    ids = ids.swapaxes(0, 1).reshape(4 * 64, CAP)
    ids = jnp.concatenate([ids[:, :8].reshape(1, -1), ids[:, 8:].reshape(1, -1)], axis=1)

    core = lax.axis_index("k").astype(jnp.int32).reshape(1)
    both, other = tower_grads(core, parts, features, w_first, w_second)
    both = both + shifted(other, "k", 1)
    both = summed_share(both, "y")
    both = summed_share(both, "x")
    for step in (1, 2, 4):
        both = both + lax.ppermute(both, "z", [(i, i ^ step) for i in range(8)])

    send = pack(item, owner, rank).reshape(256, 8, 128)
    came = exchange(send, YZXK).reshape(256 * 8, 128)
    both = to_all(both, KYX).reshape(512, 256)
    grad_table = table(came, ids).T
    return both[:256], both[256:], grad_table


def solution(mesh):
    torus = Mesh(mesh.devices.reshape(8, 4, 2, mesh.shape["grp"]), ("z", "x", "k", "y"))
    rows = ("z", "x", "k")
    placed = (
        P("y", rows, None),
        P(),
        P(),
        P("y", rows, None),
        P("y", rows),
        P("y", rows),
        P("y", rows, None),
        P("y", rows),
    )
    return jax.shard_map(step_body, mesh=torus, in_specs=placed, out_specs=(P(), P(), P(rows, "y")), check_vma=False)
```

profile of v0, /device:TPU:1, one launch (start us, length us, event | category | flops | bytes accessed | tf_op | source)
XLA Modules:
  0.0 178.0 jit_solution(4826813447453468787)
XLA Ops:
  0.7 2.0 %broadcast_in_dim.18 = bf16[8,256,256]{2,1,0:T(8,128)(2,1)} broadcast(bf16[256,256]{1,0:T(8,128)(2,1)} %bitcast.52), dimensions={1,2} | broadcast | bytes 1179648 | tf_op jit(solution)/shard_map/broadcast_in_dim | solution.py:31
  2.7 9.1 %all-to-all-start = ((bf16[8,256,256]{2,1,0:T(8,128)(2,1)}), bf16[8,256,256]{2,1,0:T(8,128)(2,1)S(1)}, u32[]{:S(2)}, u32[]{:S(2)}) async-start(bf16[8,256,256]{2,1,0:T(8,128)(2,1)} %broadcast_in_dim.18), calls=%async_computation | async-start | bytes 2097152 | tf_op jit(solution)/shard_map/all_to_all | solution.py:27
  12.3 2.8 %collective-permute-start.4 = (f32[64,16]{1,0:T(8,128)S(1)}, f32[64,16]{1,0:T(8,128)S(1)}, u32[]{:S(2)}, u32[]{:S(2)}) collective-permute-start(f32[64,16]{1,0:T(8,128)S(1)} %convert_element_type.97), channel_id=1, source_target_pairs={{0,3},{1,0},{2,1},{3,2},{4,7},{5,4},{6,5},{7,6},{8,11},{9,8},{10,9... | collective-permute-start | bytes 12296 | tf_op jit(solution)/shard_map/ppermute | solution.py:36
  21.5 2.5 %collective-permute-start.2 = (bf16[512,256]{1,0:T(8,128)(2,1)S(1)}, bf16[512,256]{1,0:T(8,128)(2,1)S(1)}, u32[]{:S(2)}, u32[]{:S(2)}) collective-permute-start(bf16[512,256]{1,0:T(8,128)(2,1)S(1)} %pad_maximum_fusion), channel_id=1, source_target_pairs={{0,16},{8,24},{16,0},{24,8},{1,17},{9,25},{17,1},{25,9},{2,18},{10... | collective-permute-start | bytes 786440 | tf_op jit(solution)/shard_map/ppermute | solution.py:36
  27.7 5.7 %collective-permute-done.2 = bf16[512,256]{1,0:T(8,128)(2,1)S(1)} collective-permute-done((bf16[512,256]{1,0:T(8,128)(2,1)S(1)}, bf16[512,256]{1,0:T(8,128)(2,1)S(1)}, u32[]{:S(2)}, u32[]{:S(2)}) %collective-permute-start.2) | collective-permute-done | bytes 262176 | tf_op jit(solution)/shard_map/ppermute | solution.py:36
  34.9 2.1 %convolution_convert_fusion.users_ref = bf16[2048,256]{1,0:T(8,128)(2,1)S(1)} fusion(bf16[256,256]{1,0:T(8,128)(2,1)S(1)} %copy-done.1, bf16[2048,256]{1,0:T(8,128)(2,1)} %constant_dynamic-update-slice_fusion, bf16[256,256]{1,0:T(8,128)(2,1)S(1)} %copy-done.2), kind=kOutput, calls=%fused_computation | convolution fusion | flops 540016640 | bytes 2359296 | tf_op jit(solution)/shard_map/dot_general | solution.py:257
  36.9 4.1 %all-to-all-done = bf16[8,256,256]{2,1,0:T(8,128)(2,1)S(1)} async-done(((bf16[8,256,256]{2,1,0:T(8,128)(2,1)}), bf16[8,256,256]{2,1,0:T(8,128)(2,1)S(1)}, u32[]{:S(2)}, u32[]{:S(2)}) %all-to-all-start) | async-done | bytes 1048608 | tf_op jit(solution)/shard_map/all_to_all | solution.py:27
  41.0 5.2 %stats.1 = f32[8,40,256]{2,1,0:T(8,128)S(1)} custom-call(s32[10]{0:T(128)S(1)} %pad_add_fusion.1.at_ref, bf16[2048,256]{1,0:T(8,128)(2,1)S(1)} %bitcast.39, bf16[2048,256]{1,0:T(8,128)(2,1)S(1)} %convolution_convert_fusion.users_ref, f32[24,256]{1,0:T(8,128)S(1)} %pad_maximum_fusion.1.own_ref), custom_call_target="tpu_custom_call" | custom-call | tf_op jit(solution)/shard_map/stats/pallas_call | solution.py:78
  46.2 12.1 %all_to_all.25.got_ref = f32[8,40,256]{2,1,0:T(8,128)S(1)} all-to-all(f32[8,40,256]{2,1,0:T(8,128)S(1)} %stats.1), channel_id=1, replica_groups=mesh['z'=8,'x'=4,'k'=2,'y'=4] {'x','k'}, dimensions={0} | all-to-all | bytes 655360 | tf_op jit(solution)/shard_map/all_to_all | solution.py:27
  58.2 6.6 %user_side.1 = (bf16[2048,2048]{1,0:T(8,128)(2,1)S(1)}, f32[4,256,256]{2,1,0:T(8,128)S(1)}, f32[4,256,256]{2,1,0:T(8,128)}) custom-call(s32[10]{0:T(128)S(1)} %pad_add_fusion.1.at_ref, bf16[2048,256]{1,0:T(8,128)(2,1)S(1)} %bitcast.40, bf16[2048,256]{1,0:T(8,128)(2,1)S(1)} %convolution_convert_fusion.users_ref, f32[8,40,256]{2,1,0:T(8,128)S(1)} %all_to_all.25.got_ref), custom_call_target="tpu_custom_call" | custom-call | tf_op jit(solution)/shard_map/user_side/pallas_call | solution.py:116
  65.6 3.0 %item_side.1 = f32[8,264,256]{2,1,0:T(8,128)S(1)} custom-call(s32[10]{0:T(128)S(1)} %pad_add_fusion.1.at_ref, bf16[2048,2048]{1,0:T(8,128)(2,1)S(1)} %get-tuple-element.12.all_ref, bf16[2048,256]{1,0:T(8,128)(2,1)S(1)} %convolution_convert_fusion.users_ref, f32[8,40,256]{2,1,0:T(8,128)S(1)} %all_to_all.25.got_ref), custom_call_target="tpu_custom_call" | custom-call | tf_op jit(solution)/shard_map/item_side/pallas_call | solution.py:150
  69.8 4.7 %all-to-all-start.3 = ((f16[8,264,256]{2,1,0:T(8,128)(2,1)}), f16[8,264,256]{2,1,0:T(8,128)(2,1)S(1)}, u32[]{:S(2)}, u32[]{:S(2)}) async-start(f16[8,264,256]{2,1,0:T(8,128)(2,1)} %convert_element_type.100), calls=%async_computation.3 | async-start | bytes 2162688 | tf_op jit(solution)/shard_map/all_to_all | solution.py:27
  78.1 5.5 %collective-permute-done.8.one_ref = f32[256,256]{1,0:T(8,128)S(1)} collective-permute-done((f32[256,256]{1,0:T(8,128)S(1)}, f32[256,256]{1,0:T(8,128)S(1)}, u32[]{:S(2)}, u32[]{:S(2)}) %collective-permute-start.8) | collective-permute-done | bytes 262176 | tf_op jit(solution)/shard_map/ppermute | solution.py:36
  83.6 2.1 %collective-permute-done.9.two_ref = f32[256,256]{1,0:T(8,128)S(1)} collective-permute-done((f32[256,256]{1,0:T(8,128)S(1)}, f32[256,256]{1,0:T(8,128)S(1)}, u32[]{:S(2)}, u32[]{:S(2)}) %collective-permute-start.9) | collective-permute-done | bytes 262176 | tf_op jit(solution)/shard_map/ppermute | solution.py:36
  85.7 6.5 %collective-permute-done.10.three_ref = f32[256,256]{1,0:T(8,128)S(1)} collective-permute-done((f32[256,256]{1,0:T(8,128)S(1)}, f32[256,256]{1,0:T(8,128)S(1)}, u32[]{:S(2)}, u32[]{:S(2)}) %collective-permute-start.10) | collective-permute-done | bytes 262176 | tf_op jit(solution)/shard_map/ppermute | solution.py:36
  98.0 3.4 %collective-permute-done.13 = f32[64,256]{1,0:T(8,128)S(1)} collective-permute-done((f32[64,256]{1,0:T(8,128)S(1)}, f32[64,256]{1,0:T(8,128)S(1)}, u32[]{:S(2)}, u32[]{:S(2)}) %collective-permute-start.13) | collective-permute-done | bytes 65568 | tf_op jit(solution)/shard_map/ppermute | solution.py:36
  111.0 2.4 %collective-permute-start.19 = (f32[16,256]{1,0:T(8,128)S(1)}, f32[16,256]{1,0:T(8,128)S(1)}, u32[]{:S(2)}, u32[]{:S(2)}) collective-permute-start(f32[16,256]{1,0:T(8,128)S(1)} %add.134), channel_id=1, source_target_pairs={{0,64},{32,96},{64,0},{96,32},{128,192},{160,224},{192,128},{224,1... | collective-permute-start | bytes 49160 | tf_op jit(solution)/shard_map/ppermute | solution.py:306
  114.5 5.5 %collective-permute-start.20 = (f32[16,256]{1,0:T(8,128)S(1)}, f32[16,256]{1,0:T(8,128)S(1)}, u32[]{:S(2)}, u32[]{:S(2)}) collective-permute-start(f32[16,256]{1,0:T(8,128)S(1)} %add.135), channel_id=1, source_target_pairs={{0,128},{32,160},{64,192},{96,224},{128,0},{160,32},{192,64},{224,... | collective-permute-start | bytes 49160 | tf_op jit(solution)/shard_map/ppermute | solution.py:306
  122.0 9.8 %all-to-all-start.2 = ((f32[32,16,256]{2,1,0:T(8,128)}), f32[32,16,256]{2,1,0:T(8,128)S(1)}, u32[]{:S(2)}, u32[]{:S(2)}) async-start(f32[32,16,256]{2,1,0:T(8,128)} %broadcast_in_dim.20), calls=%async_computation.2 | async-start | bytes 1048576 | tf_op jit(solution)/shard_map/all_to_all | solution.py:27
  132.4 5.1 %fusion.1.item_ref = bf16[256,256]{1,0:T(8,128)(2,1)S(1)} fusion(f32[]{:T(128)} %bitcast.21, f16[8,264,256]{2,1,0:T(8,128)(2,1)S(1)} %all-to-all-done.3, f32[]{:T(128)} %bitcast.20, f32[]{:T(128)} %bitcast.19, f32[]{:T(128)} %bitcast.18, f32[]{:T(128)} %bitcast.17, f32[]{:T(128)} %bitcast.16, f32[]{:T(128)} %bitcast.15, f32[]{:T(128)} %bitcast.14), kind=kLoop, calls=%fused_computation.12 | loop fusion | flops 1572864 | bytes 1179680 | tf_op jit(solution)/shard_map/convert_element_type | solution.py:294
  138.8 4.2 %all-to-all-done.2 = f32[32,16,256]{2,1,0:T(8,128)S(1)} async-done(((f32[32,16,256]{2,1,0:T(8,128)}), f32[32,16,256]{2,1,0:T(8,128)S(1)}, u32[]{:S(2)}, u32[]{:S(2)}) %all-to-all-start.2) | async-done | bytes 524320 | tf_op jit(solution)/shard_map/all_to_all | solution.py:27
  143.0 10.0 %all-to-all-start.4 = ((bf16[256,8,128]{2,1,0:T(8,128)(2,1)}), bf16[256,8,128]{2,1,0:T(8,128)(2,1)S(1)}, u32[]{:S(2)}, u32[]{:S(2)}) async-start(bf16[256,8,128]{2,1,0:T(8,128)(2,1)} %bitcast.25), calls=%async_computation.4 | async-start | bytes 1048576 | tf_op jit(solution)/shard_map/all_to_all | solution.py:27
  154.2 19.2 %all-to-all-done.4 = bf16[256,8,128]{2,1,0:T(8,128)(2,1)S(1)} async-done(((bf16[256,8,128]{2,1,0:T(8,128)(2,1)}), bf16[256,8,128]{2,1,0:T(8,128)(2,1)S(1)}, u32[]{:S(2)}, u32[]{:S(2)}) %all-to-all-start.4) | async-done | bytes 524320 | tf_op jit(solution)/shard_map/all_to_all | solution.py:27
  173.4 4.6 %table.1 = f32[64,4096]{1,0:T(8,128)} custom-call(bf16[2048,128]{1,0:T(8,128)(2,1)S(1)} %bitcast.41, s32[1,4096]{1,0:T(1,128)S(1)} %pad_add_fusion.ids_ref), custom_call_target="tpu_custom_call" | custom-call | tf_op jit(solution)/shard_map/table/pallas_call | solution.py:244
  (100 shorter events, 39.1 us)
Async XLA Ops:
  2.7 38.3 %all-to-all-start = ((bf16[8,256,256]{2,1,0:T(8,128)(2,1)}), bf16[8,256,256]{2,1,0:T(8,128)(2,1)S(1)}, u32[]{:S(2)}, u32[]{:S(2)}) async-start(bf16[8,256,256]{2,1,0:T(8,128)(2,1)} %broadcast_in_dim.18), calls=%async_computation | async-start | bytes 2097152 | tf_op jit(solution)/shard_map/all_to_all | solution.py:27
  12.3 6.5 %collective-permute-start.4 = (f32[64,16]{1,0:T(8,128)S(1)}, f32[64,16]{1,0:T(8,128)S(1)}, u32[]{:S(2)}, u32[]{:S(2)}) collective-permute-start(f32[64,16]{1,0:T(8,128)S(1)} %convert_element_type.97), channel_id=1, source_target_pairs={{0,3},{1,0},{2,1},{3,2},{4,7},{5,4},{6,5},{7,6},{8,11},{9,8},{10,9... | collective-permute-start | bytes 12296 | tf_op jit(solution)/shard_map/ppermute | solution.py:36
  15.1 4.3 %collective-permute-start.5 = (f32[64,16]{1,0:T(8,128)S(1)}, f32[64,16]{1,0:T(8,128)S(1)}, u32[]{:S(2)}, u32[]{:S(2)}) collective-permute-start(f32[64,16]{1,0:T(8,128)S(1)} %convert_element_type.97), channel_id=1, source_target_pairs={{0,2},{1,3},{2,0},{3,1},{4,6},{5,7},{6,4},{7,5},{8,10},{9,11},{10,... | collective-permute-start | bytes 12296 | tf_op jit(solution)/shard_map/ppermute | solution.py:36
  15.4 4.3 %collective-permute-start.6 = (f32[64,16]{1,0:T(8,128)S(1)}, f32[64,16]{1,0:T(8,128)S(1)}, u32[]{:S(2)}, u32[]{:S(2)}) collective-permute-start(f32[64,16]{1,0:T(8,128)S(1)} %convert_element_type.97), channel_id=1, source_target_pairs={{0,1},{1,2},{2,3},{3,0},{4,5},{5,6},{6,7},{7,4},{8,9},{9,10},{10,1... | collective-permute-start | bytes 12296 | tf_op jit(solution)/shard_map/ppermute | solution.py:36
  16.1 4.0 %collective-permute-start = (bf16[256,256]{1,0:T(8,128)(2,1)S(1)}, bf16[256,256]{1,0:T(8,128)(2,1)S(1)}, u32[]{:S(2)}, u32[]{:S(2)}) collective-permute-start(bf16[256,256]{1,0:T(8,128)(2,1)S(1)} %bitcast.42), channel_id=1, source_target_pairs={{0,4},{4,0},{1,5},{5,1},{2,6},{6,2},{3,7},{7,3},{8,12},{12,8},{9,1... | collective-permute-start | bytes 393224 | tf_op jit(solution)/shard_map/ppermute | solution.py:36
  20.2 6.8 %collective-permute-start.1 = (bf16[512,256]{1,0:T(8,128)(2,1)S(1)}, bf16[512,256]{1,0:T(8,128)(2,1)S(1)}, u32[]{:S(2)}, u32[]{:S(2)}) collective-permute-start(bf16[512,256]{1,0:T(8,128)(2,1)S(1)} %pad_maximum_fusion), channel_id=1, source_target_pairs={{0,8},{8,16},{16,24},{24,0},{1,9},{9,17},{17,25},{25,1},{2,10},{10... | collective-permute-start | bytes 786440 | tf_op jit(solution)/shard_map/ppermute | solution.py:36
  21.5 11.9 %collective-permute-start.2 = (bf16[512,256]{1,0:T(8,128)(2,1)S(1)}, bf16[512,256]{1,0:T(8,128)(2,1)S(1)}, u32[]{:S(2)}, u32[]{:S(2)}) collective-permute-start(bf16[512,256]{1,0:T(8,128)(2,1)S(1)} %pad_maximum_fusion), channel_id=1, source_target_pairs={{0,16},{8,24},{16,0},{24,8},{1,17},{9,25},{17,1},{25,9},{2,18},{10... | collective-permute-start | bytes 786440 | tf_op jit(solution)/shard_map/ppermute | solution.py:36
  24.0 10.1 %collective-permute-start.3 = (bf16[512,256]{1,0:T(8,128)(2,1)S(1)}, bf16[512,256]{1,0:T(8,128)(2,1)S(1)}, u32[]{:S(2)}, u32[]{:S(2)}) collective-permute-start(bf16[512,256]{1,0:T(8,128)(2,1)S(1)} %pad_maximum_fusion), channel_id=1, source_target_pairs={{0,24},{8,0},{16,8},{24,16},{1,25},{9,1},{17,9},{25,17},{2,26},{10... | collective-permute-start | bytes 786440 | tf_op jit(solution)/shard_map/ppermute | solution.py:36
  64.8 9.7 %collective-permute-start.7 = (f32[4,256,256]{2,1,0:T(8,128)}, f32[4,256,256]{2,1,0:T(8,128)}, u32[]{:S(2)}, u32[]{:S(2)}) collective-permute-start(f32[4,256,256]{2,1,0:T(8,128)} %get-tuple-element.9), channel_id=1, source_target_pairs={{0,4},{4,0},{1,5},{5,1},{2,6},{6,2},{3,7},{7,3},{8,12},{12,8},{9,1... | collective-permute-start | bytes 3145736 | tf_op jit(solution)/shard_map/ppermute | solution.py:36
  69.8 51.4 %all-to-all-start.3 = ((f16[8,264,256]{2,1,0:T(8,128)(2,1)}), f16[8,264,256]{2,1,0:T(8,128)(2,1)S(1)}, u32[]{:S(2)}, u32[]{:S(2)}) async-start(f16[8,264,256]{2,1,0:T(8,128)(2,1)} %convert_element_type.100), calls=%async_computation.3 | async-start | bytes 2162688 | tf_op jit(solution)/shard_map/all_to_all | solution.py:27
  75.9 7.7 %collective-permute-start.8 = (f32[256,256]{1,0:T(8,128)S(1)}, f32[256,256]{1,0:T(8,128)S(1)}, u32[]{:S(2)}, u32[]{:S(2)}) collective-permute-start(f32[256,256]{1,0:T(8,128)S(1)} %get-tuple-element.15), channel_id=1, source_target_pairs={{0,24},{8,0},{16,8},{24,16},{1,25},{9,1},{17,9},{25,17},{2,26},{10... | collective-permute-start | bytes 786440 | tf_op jit(solution)/shard_map/ppermute | solution.py:36
  76.9 8.8 %collective-permute-start.9 = (f32[256,256]{1,0:T(8,128)S(1)}, f32[256,256]{1,0:T(8,128)S(1)}, u32[]{:S(2)}, u32[]{:S(2)}) collective-permute-start(f32[256,256]{1,0:T(8,128)S(1)} %get-tuple-element.14), channel_id=1, source_target_pairs={{0,16},{8,24},{16,0},{24,8},{1,17},{9,25},{17,1},{25,9},{2,18},{10... | collective-permute-start | bytes 786440 | tf_op jit(solution)/shard_map/ppermute | solution.py:36
  78.1 14.2 %collective-permute-start.10 = (f32[256,256]{1,0:T(8,128)S(1)}, f32[256,256]{1,0:T(8,128)S(1)}, u32[]{:S(2)}, u32[]{:S(2)}) collective-permute-start(f32[256,256]{1,0:T(8,128)S(1)} %get-tuple-element.13), channel_id=1, source_target_pairs={{0,8},{8,16},{16,24},{24,0},{1,9},{9,17},{17,25},{25,1},{2,10},{10... | collective-permute-start | bytes 786440 | tf_op jit(solution)/shard_map/ppermute | solution.py:36
  94.6 3.4 %collective-permute-start.14 = (f32[64,256]{1,0:T(8,128)S(1)}, f32[64,256]{1,0:T(8,128)S(1)}, u32[]{:S(2)}, u32[]{:S(2)}) collective-permute-start(f32[64,256]{1,0:T(8,128)S(1)} %get-tuple-element.19), channel_id=1, source_target_pairs={{0,3},{1,0},{2,1},{3,2},{4,7},{5,4},{6,5},{7,6},{8,11},{9,8},{10,9... | collective-permute-start | bytes 196616 | tf_op jit(solution)/shard_map/ppermute | solution.py:36
  96.5 4.9 %collective-permute-start.13 = (f32[64,256]{1,0:T(8,128)S(1)}, f32[64,256]{1,0:T(8,128)S(1)}, u32[]{:S(2)}, u32[]{:S(2)}) collective-permute-start(f32[64,256]{1,0:T(8,128)S(1)} %get-tuple-element.20), channel_id=1, source_target_pairs={{0,2},{1,3},{2,0},{3,1},{4,6},{5,7},{6,4},{7,5},{8,10},{9,11},{10,... | collective-permute-start | bytes 196616 | tf_op jit(solution)/shard_map/ppermute | solution.py:36
  97.5 4.9 %collective-permute-start.12 = (f32[64,256]{1,0:T(8,128)S(1)}, f32[64,256]{1,0:T(8,128)S(1)}, u32[]{:S(2)}, u32[]{:S(2)}) collective-permute-start(f32[64,256]{1,0:T(8,128)S(1)} %get-tuple-element.18), channel_id=1, source_target_pairs={{0,1},{1,2},{2,3},{3,0},{4,5},{5,6},{6,7},{7,4},{8,9},{9,10},{10,1... | collective-permute-start | bytes 196616 | tf_op jit(solution)/shard_map/ppermute | solution.py:36
  102.5 2.7 %collective-permute-start.17 = (f32[16,256]{1,0:T(8,128)S(1)}, f32[16,256]{1,0:T(8,128)S(1)}, u32[]{:S(2)}, u32[]{:S(2)}) collective-permute-start(f32[16,256]{1,0:T(8,128)S(1)} %get-tuple-element.24), channel_id=1, source_target_pairs={{0,24},{8,0},{16,8},{24,16},{1,25},{9,1},{17,9},{25,17},{2,26},{10... | collective-permute-start | bytes 49160 | tf_op jit(solution)/shard_map/ppermute | solution.py:36
  102.9 4.1 %collective-permute-start.16 = (f32[16,256]{1,0:T(8,128)S(1)}, f32[16,256]{1,0:T(8,128)S(1)}, u32[]{:S(2)}, u32[]{:S(2)}) collective-permute-start(f32[16,256]{1,0:T(8,128)S(1)} %get-tuple-element.25), channel_id=1, source_target_pairs={{0,16},{8,24},{16,0},{24,8},{1,17},{9,25},{17,1},{25,9},{2,18},{10... | collective-permute-start | bytes 49160 | tf_op jit(solution)/shard_map/ppermute | solution.py:36
  104.1 3.8 %collective-permute-start.15 = (f32[16,256]{1,0:T(8,128)S(1)}, f32[16,256]{1,0:T(8,128)S(1)}, u32[]{:S(2)}, u32[]{:S(2)}) collective-permute-start(f32[16,256]{1,0:T(8,128)S(1)} %get-tuple-element.23), channel_id=1, source_target_pairs={{0,8},{8,16},{16,24},{24,0},{1,9},{9,17},{17,25},{25,1},{2,10},{10... | collective-permute-start | bytes 49160 | tf_op jit(solution)/shard_map/ppermute | solution.py:36
  107.9 3.1 %collective-permute-start.18 = (f32[16,256]{1,0:T(8,128)S(1)}, f32[16,256]{1,0:T(8,128)S(1)}, u32[]{:S(2)}, u32[]{:S(2)}) collective-permute-start(f32[16,256]{1,0:T(8,128)S(1)} %add_add_fusion.1), channel_id=1, source_target_pairs={{0,32},{32,0},{64,96},{96,64},{128,160},{160,128},{192,224},{224,1... | collective-permute-start | bytes 49160 | tf_op jit(solution)/shard_map/ppermute | solution.py:306
  111.0 3.5 %collective-permute-start.19 = (f32[16,256]{1,0:T(8,128)S(1)}, f32[16,256]{1,0:T(8,128)S(1)}, u32[]{:S(2)}, u32[]{:S(2)}) collective-permute-start(f32[16,256]{1,0:T(8,128)S(1)} %add.134), channel_id=1, source_target_pairs={{0,64},{32,96},{64,0},{96,32},{128,192},{160,224},{192,128},{224,1... | collective-permute-start | bytes 49160 | tf_op jit(solution)/shard_map/ppermute | solution.py:306
  114.5 6.7 %collective-permute-start.20 = (f32[16,256]{1,0:T(8,128)S(1)}, f32[16,256]{1,0:T(8,128)S(1)}, u32[]{:S(2)}, u32[]{:S(2)}) collective-permute-start(f32[16,256]{1,0:T(8,128)S(1)} %add.135), channel_id=1, source_target_pairs={{0,128},{32,160},{64,192},{96,224},{128,0},{160,32},{192,64},{224,... | collective-permute-start | bytes 49160 | tf_op jit(solution)/shard_map/ppermute | solution.py:306
  122.0 20.9 %all-to-all-start.2 = ((f32[32,16,256]{2,1,0:T(8,128)}), f32[32,16,256]{2,1,0:T(8,128)S(1)}, u32[]{:S(2)}, u32[]{:S(2)}) async-start(f32[32,16,256]{2,1,0:T(8,128)} %broadcast_in_dim.20), calls=%async_computation.2 | async-start | bytes 1048576 | tf_op jit(solution)/shard_map/all_to_all | solution.py:27
  143.0 30.5 %all-to-all-start.4 = ((bf16[256,8,128]{2,1,0:T(8,128)(2,1)}), bf16[256,8,128]{2,1,0:T(8,128)(2,1)S(1)}, u32[]{:S(2)}, u32[]{:S(2)}) async-start(bf16[256,8,128]{2,1,0:T(8,128)(2,1)} %bitcast.25), calls=%async_computation.4 | async-start | bytes 1048576 | tf_op jit(solution)/shard_map/all_to_all | solution.py:27
  (8 other events, 125.0 us)
where the time goes:
time: 179 us; the launch traced here: 178 us
  starting transfers between devices  62.5 us (35%)
  waiting for transfers between devices  61.9 us (35%)
  Pallas kernels  21.1 us (12%)
  blocking collectives  12.1 us (7%)
  local copies, waits for them, and re-layouts  9.03 us (5%)
  other arithmetic  8.22 us (5%)
  matrix products  2.23 us (1%)
    all_to_all x4, starting transfers between devices, exchange(): return lax.all_to_all(value, axes, 0, 0, tiled=True)  33.6 us
    ppermute x18, waiting for transfers between devices, shifted(): lax.ppermute(value, axis, [(i, (i + step) % count) for i in range(count)])  31.1 us
    all_to_all x4, waiting for transfers between devices, exchange(): return lax.all_to_all(value, axes, 0, 0, tiled=True)  27.4 us
    ppermute x18, starting transfers between devices, shifted(): lax.ppermute(value, axis, [(i, (i + step) % count) for i in range(count)])  19.1 us
    all_to_all x1, blocking collectives, exchange(): return lax.all_to_all(value, axes, 0, 0, tiled=True)  12.1 us
    ppermute x3, starting transfers between devices, step_body(): both = both + lax.ppermute(both, 'z', [(i, i ^ step) for i in range(8)])  9.86 us
    pallas_call x1, Pallas kernels, user_side(): pl.pallas_call(users_kernel, in_specs=[SMEM, VMEM, VMEM, VMEM], out_specs...  6.61 us
    pallas_call x1, Pallas kernels, stats(): pl.pallas_call(stats_kernel, in_specs=[SMEM, VMEM, VMEM, VMEM], out_shape...  5.18 us
  transfers between devices with their start and end apart: 25, of which 20 were waited for; matrix products, arithmetic and copies ran while one was open for 9% of the time, Pallas kernels for 3%

commit v1 on v0

--- a/solution.py
+++ b/solution.py
@@ -125,25 +125,24 @@
 
 
 def items_kernel(at_ref, all_ref, users_ref, got_ref, gi_ref, ids_ref):
-    largest = jnp.max(jnp.abs(users_ref[...].astype(F32)), axis=0, keepdims=True)
-    largest = jnp.maximum(jnp.max(largest, axis=1, keepdims=True) * 416.0, 1e-30)
-    power = jnp.ceil(jnp.log(largest) * 1.4426950408889634)
-    gi = dot(all_ref[...], users_ref[...], (1, 0)) * jnp.exp2(15.0 - power)
+    gi = dot(all_ref[...], users_ref[...], (1, 0))
+    ids_ref[...] = jnp.zeros_like(ids_ref)
     for z in range(8):
-        gi_ref[z, :BLK, :] = gi[z * BLK : (z + 1) * BLK]
+        part = gi[z * BLK : (z + 1) * BLK]
+        largest = jnp.maximum(jnp.max(jnp.abs(part), axis=0, keepdims=True), 1e-30)
+        power = jnp.ceil(jnp.log(largest) * 1.4426950408889634)
+        whole = jnp.floor(part * jnp.exp2(14.9 - power) + 0.5)
+        gi_ref[z, :BLK, :] = whole.astype(jnp.int32).astype(jnp.int16)
+        ids_ref[z, 4:5, :] = power
     lane = lax.broadcasted_iota(jnp.int32, (8, 128), 1) // CAP
-    ids_ref[...] = jnp.zeros_like(ids_ref)
     for y in range(4):
         row = jnp.zeros((8, 128), F32)
         for p in range(8):
             piece = got_ref[p, 24 + 8 * (y // 2) : 32 + 8 * (y // 2), 128 * (y % 2) : 128 * (y % 2) + 128]
             turn = ((p - at_ref[9]) & 7) * CAP
             row = jnp.where(lane == p, pltpu.roll(piece, turn, 1), row)
-        high = jnp.floor(row * (1.0 / 64.0))
-        ids_ref[:, y, :128] = high
-        ids_ref[:, y, 128:] = row - 64.0 * high
-    ids_ref[:, 4, :] = jnp.broadcast_to(power, (8, 256))
-    gi_ref[:, BLK:, :] = ids_ref[...]
+        ids_ref[:, y, :128] = row
+    gi_ref[:, BLK:, :] = ids_ref[...].astype(jnp.int32).astype(jnp.int16)
 
 
 def item_side(at, dscore, users, got):
@@ -151,7 +150,7 @@
         items_kernel,
         in_specs=[SMEM, VMEM, VMEM, VMEM],
         out_specs=VMEM,
-        out_shape=jax.ShapeDtypeStruct((8, BLK + 8, 256), F32),
+        out_shape=jax.ShapeDtypeStruct((8, BLK + 8, 256), jnp.int16),
         scratch_shapes=[pltpu.VMEM((8, 8, 256), F32)],
         compiler_params=pltpu.CompilerParams(vmem_limit_bytes=22 * 2**20),
         name="item_side",
@@ -194,14 +193,19 @@
     )(core, *parts, features, w_first, w_second)
 
 
-def pack_kernel(item_ref, owner_ref, rank_ref, out_ref):
+def pack_kernel(parts_ref, owner_ref, rank_ref, out_ref):
+    item = jnp.zeros((BLK, 256), F32)
+    for z in range(8):
+        power = parts_ref[z, BLK : BLK + 8, :].astype(jnp.int32).astype(F32)[4:5]
+        item += parts_ref[z, :BLK, :].astype(jnp.int32).astype(F32) * jnp.exp2(power - 14.9)
+    item = item.astype(BF16)
     lane = lax.broadcasted_iota(jnp.int32, (64 * 8, BLK), 0)
     halves = []
     for h in range(2):
         rank = rank_ref[...] - 8 * h
         slot = jnp.where((rank >= 0) & (rank < 8), owner_ref[...] * 8 + rank, -1)
         pick = (lane == slot).astype(F32).astype(BF16)
-        halves.append(dot(pick, item_ref[...], (1, 0)))
+        halves.append(dot(pick, item, (1, 0)))
     for g in range(4):
         share = slice(64 * g, 64 * g + 64)
         both = jnp.concatenate([halves[0][:, share], halves[1][:, share]], axis=1)
@@ -287,13 +291,14 @@
     dscore, keep, give = user_side(at, items, users, got)
     swapped = shifted(give, "k", 1)
     gi = item_side(at, dscore, users, got)
-    gi = exchange(gi.astype(jnp.float16), "z")
+    gi = exchange(gi, "z")
+    gu = keep + swapped
+    parts = [gu] + [shifted(gu[d], "x", -d) for d in range(1, 4)]
     gu = keep + swapped
     parts = [gu] + [shifted(gu[d], "x", -d) for d in range(1, 4)]
     scale = jnp.exp2(gi[:, BLK + 4, 0].astype(F32) - 15.0)
     item = sum(gi[z, :BLK].astype(F32) * scale[z] for z in range(8)).astype(BF16)
-    ids = gi[:, BLK : BLK + 4, :].astype(F32)
-    ids = (64.0 * ids[:, :, :128] + ids[:, :, 128:]).astype(jnp.int32) - 1
+    ids = gi[:, BLK : BLK + 4, :128].astype(jnp.int32) - 1
     ids = ids.swapaxes(0, 1).reshape(4 * 64, CAP)
     ids = jnp.concatenate([ids[:, :8].reshape(1, -1), ids[:, 8:].reshape(1, -1)], axis=1)
 
@@ -302,10 +307,10 @@
     both = both + shifted(other, "k", 1)
     both = summed_share(both, "y")
     both = summed_share(both, "x")
-    for step in (1, 2, 4):
-        both = both + lax.ppermute(both, "z", [(i, i ^ step) for i in range(8)])
-
-    send = pack(item, owner, rank).reshape(256, 8, 128)
+    both = both + lax.ppermute(both, "z", [(i, i ^ 1) for i in range(8)])
+    both = both + sum(lax.ppermute(both, "z", [(i, i ^ step) for i in range(8)]) for step in (2, 4, 6))
+
+    send = pack(gi, owner, rank).reshape(256, 8, 128)
     came = exchange(send, YZXK).reshape(256 * 8, 128)
     both = to_all(both, KYX).reshape(512, 256)
     grad_table = table(came, ids).T

time: 179 us -> 177 us (0.989)
  waiting for transfers between devices: 61.9 us -> 71.9 us
  starting transfers between devices: 62.5 us -> 56 us
  other arithmetic: 8.22 us -> 1.85 us
  Pallas kernels: 21.1 us -> 22.9 us
    convert_element_type x3 -> x0, other arithmetic: 6.34 us -> none  [the longest x1 5.14 us: step_body(): sum((gi[z, :BLK].astype(F32) * scale[z] for z in range(8))).astype(BF16)]
    all_to_all x4, waiting for transfers between devices: 27.4 us -> 33.1 us  [exchange(): return lax.all_to_all(value, axes, 0, 0, tiled=True)]
    all_to_all x4, starting transfers between devices: 33.6 us -> 29.2 us  [exchange(): return lax.all_to_all(value, axes, 0, 0, tiled=True)]
    ppermute x3 -> x4, waiting for transfers between devices: 3.38 us -> 7.71 us  [the longest x3 6.58 us: step_body(): lax.ppermute(both, 'z', [(i, i ^ step) for i in range(8)])]
    ppermute x3 -> x4, starting transfers between devices: 9.86 us -> 7.7 us  [the longest x3 5.75 us: step_body(): lax.ppermute(both, 'z', [(i, i ^ step) for i in range(8)])]
  transfers between devices with their start and end apart: 25 -> 26, of which waited for: 20 -> 20; matrix products, arithmetic and copies ran while one was open for 9% -> 5% of each run, Pallas kernels for 3% -> 4%
where the time goes in v1:
time: 177 us; the launch traced here: 176 us
  waiting for transfers between devices  71.9 us (41%)
  starting transfers between devices  56 us (32%)
  Pallas kernels  22.9 us (13%)
  blocking collectives  12.1 us (7%)
  local copies, waits for them, and re-layouts  8.44 us (5%)
  matrix products  2.23 us (1%)
  other arithmetic  1.85 us (1%)
    all_to_all x4, waiting for transfers between devices, exchange(): return lax.all_to_all(value, axes, 0, 0, tiled=True)  33.1 us
    ppermute x18, waiting for transfers between devices, shifted(): lax.ppermute(value, axis, [(i, (i + step) % count) for i in range(count)])  31.1 us
    all_to_all x4, starting transfers between devices, exchange(): return lax.all_to_all(value, axes, 0, 0, tiled=True)  29.2 us
    ppermute x18, starting transfers between devices, shifted(): lax.ppermute(value, axis, [(i, (i + step) % count) for i in range(count)])  19.1 us
    all_to_all x1, blocking collectives, exchange(): return lax.all_to_all(value, axes, 0, 0, tiled=True)  12.1 us
    pallas_call x1, Pallas kernels, user_side(): pl.pallas_call(users_kernel, in_specs=[SMEM, VMEM, VMEM, VMEM], out_specs...  6.61 us
    ppermute x3, waiting for transfers between devices, step_body(): lax.ppermute(both, 'z', [(i, i ^ step) for i in range(8)])  6.58 us
    ppermute x3, starting transfers between devices, step_body(): lax.ppermute(both, 'z', [(i, i ^ step) for i in range(8)])  5.75 us
  transfers between devices with their start and end apart: 26, of which 20 were waited for; matrix products, arithmetic and copies ran while one was open for 5% of the time, Pallas kernels for 4%

profile of v1, /device:TPU:1, one launch (start us, length us, event | category | flops | bytes accessed | tf_op | source)
XLA Modules:
  0.0 176.3 jit_solution(2982142791535005387)
XLA Ops:
  0.7 2.0 %broadcast_in_dim.18 = bf16[8,256,256]{2,1,0:T(8,128)(2,1)} broadcast(bf16[256,256]{1,0:T(8,128)(2,1)} %bitcast.42), dimensions={1,2} | broadcast | bytes 1179648 | tf_op jit(solution)/shard_map/broadcast_in_dim | solution.py:31
  2.7 9.1 %all-to-all-start = ((bf16[8,256,256]{2,1,0:T(8,128)(2,1)}), bf16[8,256,256]{2,1,0:T(8,128)(2,1)S(1)}, u32[]{:S(2)}, u32[]{:S(2)}) async-start(bf16[8,256,256]{2,1,0:T(8,128)(2,1)} %broadcast_in_dim.18), calls=%async_computation | async-start | bytes 2097152 | tf_op jit(solution)/shard_map/all_to_all | solution.py:27
  12.3 2.8 %collective-permute-start.4 = (f32[64,16]{1,0:T(8,128)S(1)}, f32[64,16]{1,0:T(8,128)S(1)}, u32[]{:S(2)}, u32[]{:S(2)}) collective-permute-start(f32[64,16]{1,0:T(8,128)S(1)} %convert_element_type.52), channel_id=1, source_target_pairs={{0,3},{1,0},{2,1},{3,2},{4,7},{5,4},{6,5},{7,6},{8,11},{9,8},{10,9... | collective-permute-start | bytes 12296 | tf_op jit(solution)/shard_map/ppermute | solution.py:36
  21.5 2.5 %collective-permute-start.2 = (bf16[512,256]{1,0:T(8,128)(2,1)S(1)}, bf16[512,256]{1,0:T(8,128)(2,1)S(1)}, u32[]{:S(2)}, u32[]{:S(2)}) collective-permute-start(bf16[512,256]{1,0:T(8,128)(2,1)S(1)} %pad_maximum_fusion), channel_id=1, source_target_pairs={{0,16},{8,24},{16,0},{24,8},{1,17},{9,25},{17,1},{25,9},{2,18},{10... | collective-permute-start | bytes 786440 | tf_op jit(solution)/shard_map/ppermute | solution.py:36
  27.7 5.7 %collective-permute-done.2 = bf16[512,256]{1,0:T(8,128)(2,1)S(1)} collective-permute-done((bf16[512,256]{1,0:T(8,128)(2,1)S(1)}, bf16[512,256]{1,0:T(8,128)(2,1)S(1)}, u32[]{:S(2)}, u32[]{:S(2)}) %collective-permute-start.2) | collective-permute-done | bytes 262176 | tf_op jit(solution)/shard_map/ppermute | solution.py:36
  34.9 2.1 %convolution_convert_fusion.users_ref = bf16[2048,256]{1,0:T(8,128)(2,1)S(1)} fusion(bf16[256,256]{1,0:T(8,128)(2,1)S(1)} %copy-done.1, bf16[2048,256]{1,0:T(8,128)(2,1)} %constant_dynamic-update-slice_fusion, bf16[256,256]{1,0:T(8,128)(2,1)S(1)} %copy-done.2), kind=kOutput, calls=%fused_computation | convolution fusion | flops 540016640 | bytes 2359296 | tf_op jit(solution)/shard_map/dot_general | solution.py:261
  36.9 4.1 %all-to-all-done = bf16[8,256,256]{2,1,0:T(8,128)(2,1)S(1)} async-done(((bf16[8,256,256]{2,1,0:T(8,128)(2,1)}), bf16[8,256,256]{2,1,0:T(8,128)(2,1)S(1)}, u32[]{:S(2)}, u32[]{:S(2)}) %all-to-all-start) | async-done | bytes 1048608 | tf_op jit(solution)/shard_map/all_to_all | solution.py:27
  41.0 5.2 %stats.1 = f32[8,40,256]{2,1,0:T(8,128)S(1)} custom-call(s32[10]{0:T(128)S(1)} %pad_add_fusion.1.at_ref, bf16[2048,256]{1,0:T(8,128)(2,1)S(1)} %bitcast.29, bf16[2048,256]{1,0:T(8,128)(2,1)S(1)} %convolution_convert_fusion.users_ref, f32[24,256]{1,0:T(8,128)S(1)} %pad_maximum_fusion.1.own_ref), custom_call_target="tpu_custom_call" | custom-call | tf_op jit(solution)/shard_map/stats/pallas_call | solution.py:78
  46.2 12.1 %all_to_all.25.got_ref = f32[8,40,256]{2,1,0:T(8,128)S(1)} all-to-all(f32[8,40,256]{2,1,0:T(8,128)S(1)} %stats.1), channel_id=1, replica_groups=mesh['z'=8,'x'=4,'k'=2,'y'=4] {'x','k'}, dimensions={0} | all-to-all | bytes 655360 | tf_op jit(solution)/shard_map/all_to_all | solution.py:27
  58.2 6.6 %user_side.1 = (bf16[2048,2048]{1,0:T(8,128)(2,1)S(1)}, f32[4,256,256]{2,1,0:T(8,128)S(1)}, f32[4,256,256]{2,1,0:T(8,128)}) custom-call(s32[10]{0:T(128)S(1)} %pad_add_fusion.1.at_ref, bf16[2048,256]{1,0:T(8,128)(2,1)S(1)} %bitcast.30, bf16[2048,256]{1,0:T(8,128)(2,1)S(1)} %convolution_convert_fusion.users_ref, f32[8,40,256]{2,1,0:T(8,128)S(1)} %all_to_all.25.got_ref), custom_call_target="tpu_custom_call" | custom-call | tf_op jit(solution)/shard_map/user_side/pallas_call | solution.py:116
  65.6 4.5 %item_side.1 = s16[8,264,256]{2,1,0:T(8,128)(2,1)} custom-call(s32[10]{0:T(128)S(1)} %pad_add_fusion.1.at_ref, bf16[2048,2048]{1,0:T(8,128)(2,1)S(1)} %get-tuple-element.12.all_ref, bf16[2048,256]{1,0:T(8,128)(2,1)S(1)} %convolution_convert_fusion.users_ref, f32[8,40,256]{2,1,0:T(8,128)S(1)} %all_to_all.25.got_ref), custom_call_target="tpu_custom_call" | custom-call | tf_op jit(solution)/shard_map/item_side/pallas_call | solution.py:149
  70.1 4.7 %all-to-all-start.3 = ((s16[8,264,256]{2,1,0:T(8,128)(2,1)}), s16[8,264,256]{2,1,0:T(8,128)(2,1)S(1)}, u32[]{:S(2)}, u32[]{:S(2)}) async-start(s16[8,264,256]{2,1,0:T(8,128)(2,1)} %item_side.1), calls=%async_computation.3 | async-start | bytes 2162688 | tf_op jit(solution)/shard_map/all_to_all | solution.py:27
  78.4 5.5 %collective-permute-done.8.one_ref = f32[256,256]{1,0:T(8,128)S(1)} collective-permute-done((f32[256,256]{1,0:T(8,128)S(1)}, f32[256,256]{1,0:T(8,128)S(1)}, u32[]{:S(2)}, u32[]{:S(2)}) %collective-permute-start.8) | collective-permute-done | bytes 262176 | tf_op jit(solution)/shard_map/ppermute | solution.py:36
  83.9 2.1 %collective-permute-done.9.two_ref = f32[256,256]{1,0:T(8,128)S(1)} collective-permute-done((f32[256,256]{1,0:T(8,128)S(1)}, f32[256,256]{1,0:T(8,128)S(1)}, u32[]{:S(2)}, u32[]{:S(2)}) %collective-permute-start.9) | collective-permute-done | bytes 262176 | tf_op jit(solution)/shard_map/ppermute | solution.py:36
  86.1 6.5 %collective-permute-done.10.three_ref = f32[256,256]{1,0:T(8,128)S(1)} collective-permute-done((f32[256,256]{1,0:T(8,128)S(1)}, f32[256,256]{1,0:T(8,128)S(1)}, u32[]{:S(2)}, u32[]{:S(2)}) %collective-permute-start.10) | collective-permute-done | bytes 262176 | tf_op jit(solution)/shard_map/ppermute | solution.py:36
  98.4 3.4 %collective-permute-done.13 = f32[64,256]{1,0:T(8,128)S(1)} collective-permute-done((f32[64,256]{1,0:T(8,128)S(1)}, f32[64,256]{1,0:T(8,128)S(1)}, u32[]{:S(2)}, u32[]{:S(2)}) %collective-permute-start.13) | collective-permute-done | bytes 65568 | tf_op jit(solution)/shard_map/ppermute | solution.py:36
  111.3 3.6 %collective-permute-start.21 = (f32[16,256]{1,0:T(8,128)S(1)}, f32[16,256]{1,0:T(8,128)S(1)}, u32[]{:S(2)}, u32[]{:S(2)}) collective-permute-start(f32[16,256]{1,0:T(8,128)S(1)} %add.107), channel_id=1, source_target_pairs={{0,192},{32,224},{64,128},{96,160},{128,64},{160,96},{192,0},{224,... | collective-permute-start | bytes 49160 | tf_op jit(solution)/shard_map/ppermute | solution.py:311
  114.9 2.1 %collective-permute-start.19 = (f32[16,256]{1,0:T(8,128)S(1)}, f32[16,256]{1,0:T(8,128)S(1)}, u32[]{:S(2)}, u32[]{:S(2)}) collective-permute-start(f32[16,256]{1,0:T(8,128)S(1)} %add.107), channel_id=1, source_target_pairs={{0,64},{32,96},{64,0},{96,32},{128,192},{160,224},{192,128},{224,1... | collective-permute-start | bytes 49160 | tf_op jit(solution)/shard_map/ppermute | solution.py:311
  118.6 5.1 %collective-permute-done.20 = f32[16,256]{1,0:T(8,128)S(1)} collective-permute-done((f32[16,256]{1,0:T(8,128)S(1)}, f32[16,256]{1,0:T(8,128)S(1)}, u32[]{:S(2)}, u32[]{:S(2)}) %collective-permute-start.20) | collective-permute-done | bytes 16416 | tf_op jit(solution)/shard_map/ppermute | solution.py:311
  124.5 9.3 %all-to-all-start.2 = ((f32[32,16,256]{2,1,0:T(8,128)}), f32[32,16,256]{2,1,0:T(8,128)S(1)}, u32[]{:S(2)}, u32[]{:S(2)}) async-start(f32[32,16,256]{2,1,0:T(8,128)} %broadcast_in_dim.20), calls=%async_computation.2 | async-start | bytes 1048576 | tf_op jit(solution)/shard_map/all_to_all | solution.py:27
  135.3 9.7 %all-to-all-done.2 = f32[32,16,256]{2,1,0:T(8,128)S(1)} async-done(((f32[32,16,256]{2,1,0:T(8,128)}), f32[32,16,256]{2,1,0:T(8,128)S(1)}, u32[]{:S(2)}, u32[]{:S(2)}) %all-to-all-start.2) | async-done | bytes 524320 | tf_op jit(solution)/shard_map/all_to_all | solution.py:27
  145.0 6.1 %all-to-all-start.4 = ((bf16[256,8,128]{2,1,0:T(8,128)(2,1)}), bf16[256,8,128]{2,1,0:T(8,128)(2,1)S(1)}, u32[]{:S(2)}, u32[]{:S(2)}) async-start(bf16[256,8,128]{2,1,0:T(8,128)(2,1)} %bitcast.16), calls=%async_computation.4 | async-start | bytes 1048576 | tf_op jit(solution)/shard_map/all_to_all | solution.py:27
  152.4 19.3 %all-to-all-done.4 = bf16[256,8,128]{2,1,0:T(8,128)(2,1)S(1)} async-done(((bf16[256,8,128]{2,1,0:T(8,128)(2,1)}), bf16[256,8,128]{2,1,0:T(8,128)(2,1)S(1)}, u32[]{:S(2)}, u32[]{:S(2)}) %all-to-all-start.4) | async-done | bytes 524320 | tf_op jit(solution)/shard_map/all_to_all | solution.py:27
  171.7 4.6 %table.1 = f32[64,4096]{1,0:T(8,128)} custom-call(bf16[2048,128]{1,0:T(8,128)(2,1)S(1)} %bitcast.31, s32[1,4096]{1,0:T(1,128)S(1)} %pad_add_fusion.ids_ref), custom_call_target="tpu_custom_call" | custom-call | tf_op jit(solution)/shard_map/table/pallas_call | solution.py:248
  (96 shorter events, 36.8 us)
Async XLA Ops:
  2.7 38.3 %all-to-all-start = ((bf16[8,256,256]{2,1,0:T(8,128)(2,1)}), bf16[8,256,256]{2,1,0:T(8,128)(2,1)S(1)}, u32[]{:S(2)}, u32[]{:S(2)}) async-start(bf16[8,256,256]{2,1,0:T(8,128)(2,1)} %broadcast_in_dim.18), calls=%async_computation | async-start | bytes 2097152 | tf_op jit(solution)/shard_map/all_to_all | solution.py:27
  12.3 6.5 %collective-permute-start.4 = (f32[64,16]{1,0:T(8,128)S(1)}, f32[64,16]{1,0:T(8,128)S(1)}, u32[]{:S(2)}, u32[]{:S(2)}) collective-permute-start(f32[64,16]{1,0:T(8,128)S(1)} %convert_element_type.52), channel_id=1, source_target_pairs={{0,3},{1,0},{2,1},{3,2},{4,7},{5,4},{6,5},{7,6},{8,11},{9,8},{10,9... | collective-permute-start | bytes 12296 | tf_op jit(solution)/shard_map/ppermute | solution.py:36
  15.1 4.3 %collective-permute-start.5 = (f32[64,16]{1,0:T(8,128)S(1)}, f32[64,16]{1,0:T(8,128)S(1)}, u32[]{:S(2)}, u32[]{:S(2)}) collective-permute-start(f32[64,16]{1,0:T(8,128)S(1)} %convert_element_type.52), channel_id=1, source_target_pairs={{0,2},{1,3},{2,0},{3,1},{4,6},{5,7},{6,4},{7,5},{8,10},{9,11},{10,... | collective-permute-start | bytes 12296 | tf_op jit(solution)/shard_map/ppermute | solution.py:36
  15.4 4.3 %collective-permute-start.6 = (f32[64,16]{1,0:T(8,128)S(1)}, f32[64,16]{1,0:T(8,128)S(1)}, u32[]{:S(2)}, u32[]{:S(2)}) collective-permute-start(f32[64,16]{1,0:T(8,128)S(1)} %convert_element_type.52), channel_id=1, source_target_pairs={{0,1},{1,2},{2,3},{3,0},{4,5},{5,6},{6,7},{7,4},{8,9},{9,10},{10,1... | collective-permute-start | bytes 12296 | tf_op jit(solution)/shard_map/ppermute | solution.py:36
  16.1 4.0 %collective-permute-start = (bf16[256,256]{1,0:T(8,128)(2,1)S(1)}, bf16[256,256]{1,0:T(8,128)(2,1)S(1)}, u32[]{:S(2)}, u32[]{:S(2)}) collective-permute-start(bf16[256,256]{1,0:T(8,128)(2,1)S(1)} %bitcast.32), channel_id=1, source_target_pairs={{0,4},{4,0},{1,5},{5,1},{2,6},{6,2},{3,7},{7,3},{8,12},{12,8},{9,1... | collective-permute-start | bytes 393224 | tf_op jit(solution)/shard_map/ppermute | solution.py:36
  20.2 6.8 %collective-permute-start.1 = (bf16[512,256]{1,0:T(8,128)(2,1)S(1)}, bf16[512,256]{1,0:T(8,128)(2,1)S(1)}, u32[]{:S(2)}, u32[]{:S(2)}) collective-permute-start(bf16[512,256]{1,0:T(8,128)(2,1)S(1)} %pad_maximum_fusion), channel_id=1, source_target_pairs={{0,8},{8,16},{16,24},{24,0},{1,9},{9,17},{17,25},{25,1},{2,10},{10... | collective-permute-start | bytes 786440 | tf_op jit(solution)/shard_map/ppermute | solution.py:36
  21.5 11.9 %collective-permute-start.2 = (bf16[512,256]{1,0:T(8,128)(2,1)S(1)}, bf16[512,256]{1,0:T(8,128)(2,1)S(1)}, u32[]{:S(2)}, u32[]{:S(2)}) collective-permute-start(bf16[512,256]{1,0:T(8,128)(2,1)S(1)} %pad_maximum_fusion), channel_id=1, source_target_pairs={{0,16},{8,24},{16,0},{24,8},{1,17},{9,25},{17,1},{25,9},{2,18},{10... | collective-permute-start | bytes 786440 | tf_op jit(solution)/shard_map/ppermute | solution.py:36
  24.0 10.1 %collective-permute-start.3 = (bf16[512,256]{1,0:T(8,128)(2,1)S(1)}, bf16[512,256]{1,0:T(8,128)(2,1)S(1)}, u32[]{:S(2)}, u32[]{:S(2)}) collective-permute-start(bf16[512,256]{1,0:T(8,128)(2,1)S(1)} %pad_maximum_fusion), channel_id=1, source_target_pairs={{0,24},{8,0},{16,8},{24,16},{1,25},{9,1},{17,9},{25,17},{2,26},{10... | collective-permute-start | bytes 786440 | tf_op jit(solution)/shard_map/ppermute | solution.py:36
  64.8 10.0 %collective-permute-start.7 = (f32[4,256,256]{2,1,0:T(8,128)}, f32[4,256,256]{2,1,0:T(8,128)}, u32[]{:S(2)}, u32[]{:S(2)}) collective-permute-start(f32[4,256,256]{2,1,0:T(8,128)} %get-tuple-element.9), channel_id=1, source_target_pairs={{0,4},{4,0},{1,5},{5,1},{2,6},{6,2},{3,7},{7,3},{8,12},{12,8},{9,1... | collective-permute-start | bytes 3145736 | tf_op jit(solution)/shard_map/ppermute | solution.py:36
  70.1 53.5 %all-to-all-start.3 = ((s16[8,264,256]{2,1,0:T(8,128)(2,1)}), s16[8,264,256]{2,1,0:T(8,128)(2,1)S(1)}, u32[]{:S(2)}, u32[]{:S(2)}) async-start(s16[8,264,256]{2,1,0:T(8,128)(2,1)} %item_side.1), calls=%async_computation.3 | async-start | bytes 2162688 | tf_op jit(solution)/shard_map/all_to_all | solution.py:27
  76.2 7.7 %collective-permute-start.8 = (f32[256,256]{1,0:T(8,128)S(1)}, f32[256,256]{1,0:T(8,128)S(1)}, u32[]{:S(2)}, u32[]{:S(2)}) collective-permute-start(f32[256,256]{1,0:T(8,128)S(1)} %get-tuple-element.15), channel_id=1, source_target_pairs={{0,24},{8,0},{16,8},{24,16},{1,25},{9,1},{17,9},{25,17},{2,26},{10... | collective-permute-start | bytes 786440 | tf_op jit(solution)/shard_map/ppermute | solution.py:36
  77.2 8.8 %collective-permute-start.9 = (f32[256,256]{1,0:T(8,128)S(1)}, f32[256,256]{1,0:T(8,128)S(1)}, u32[]{:S(2)}, u32[]{:S(2)}) collective-permute-start(f32[256,256]{1,0:T(8,128)S(1)} %get-tuple-element.14), channel_id=1, source_target_pairs={{0,16},{8,24},{16,0},{24,8},{1,17},{9,25},{17,1},{25,9},{2,18},{10... | collective-permute-start | bytes 786440 | tf_op jit(solution)/shard_map/ppermute | solution.py:36
  78.4 14.2 %collective-permute-start.10 = (f32[256,256]{1,0:T(8,128)S(1)}, f32[256,256]{1,0:T(8,128)S(1)}, u32[]{:S(2)}, u32[]{:S(2)}) collective-permute-start(f32[256,256]{1,0:T(8,128)S(1)} %get-tuple-element.13), channel_id=1, source_target_pairs={{0,8},{8,16},{16,24},{24,0},{1,9},{9,17},{17,25},{25,1},{2,10},{10... | collective-permute-start | bytes 786440 | tf_op jit(solution)/shard_map/ppermute | solution.py:36
  94.9 3.4 %collective-permute-start.14 = (f32[64,256]{1,0:T(8,128)S(1)}, f32[64,256]{1,0:T(8,128)S(1)}, u32[]{:S(2)}, u32[]{:S(2)}) collective-permute-start(f32[64,256]{1,0:T(8,128)S(1)} %get-tuple-element.19), channel_id=1, source_target_pairs={{0,3},{1,0},{2,1},{3,2},{4,7},{5,4},{6,5},{7,6},{8,11},{9,8},{10,9... | collective-permute-start | bytes 196616 | tf_op jit(solution)/shard_map/ppermute | solution.py:36
  96.9 4.9 %collective-permute-start.13 = (f32[64,256]{1,0:T(8,128)S(1)}, f32[64,256]{1,0:T(8,128)S(1)}, u32[]{:S(2)}, u32[]{:S(2)}) collective-permute-start(f32[64,256]{1,0:T(8,128)S(1)} %get-tuple-element.20), channel_id=1, source_target_pairs={{0,2},{1,3},{2,0},{3,1},{4,6},{5,7},{6,4},{7,5},{8,10},{9,11},{10,... | collective-permute-start | bytes 196616 | tf_op jit(solution)/shard_map/ppermute | solution.py:36
  97.9 4.9 %collective-permute-start.12 = (f32[64,256]{1,0:T(8,128)S(1)}, f32[64,256]{1,0:T(8,128)S(1)}, u32[]{:S(2)}, u32[]{:S(2)}) collective-permute-start(f32[64,256]{1,0:T(8,128)S(1)} %get-tuple-element.18), channel_id=1, source_target_pairs={{0,1},{1,2},{2,3},{3,0},{4,5},{5,6},{6,7},{7,4},{8,9},{9,10},{10,1... | collective-permute-start | bytes 196616 | tf_op jit(solution)/shard_map/ppermute | solution.py:36
  103.2 4.1 %collective-permute-start.16 = (f32[16,256]{1,0:T(8,128)S(1)}, f32[16,256]{1,0:T(8,128)S(1)}, u32[]{:S(2)}, u32[]{:S(2)}) collective-permute-start(f32[16,256]{1,0:T(8,128)S(1)} %get-tuple-element.25), channel_id=1, source_target_pairs={{0,16},{8,24},{16,0},{24,8},{1,17},{9,25},{17,1},{25,9},{2,18},{10... | collective-permute-start | bytes 49160 | tf_op jit(solution)/shard_map/ppermute | solution.py:36
  104.4 3.8 %collective-permute-start.15 = (f32[16,256]{1,0:T(8,128)S(1)}, f32[16,256]{1,0:T(8,128)S(1)}, u32[]{:S(2)}, u32[]{:S(2)}) collective-permute-start(f32[16,256]{1,0:T(8,128)S(1)} %get-tuple-element.23), channel_id=1, source_target_pairs={{0,8},{8,16},{16,24},{24,0},{1,9},{9,17},{17,25},{25,1},{2,10},{10... | collective-permute-start | bytes 49160 | tf_op jit(solution)/shard_map/ppermute | solution.py:36
  108.2 3.1 %collective-permute-start.18 = (f32[16,256]{1,0:T(8,128)S(1)}, f32[16,256]{1,0:T(8,128)S(1)}, u32[]{:S(2)}, u32[]{:S(2)}) collective-permute-start(f32[16,256]{1,0:T(8,128)S(1)} %add_add_fusion.2), channel_id=1, source_target_pairs={{0,32},{32,0},{64,96},{96,64},{128,160},{160,128},{192,224},{224,1... | collective-permute-start | bytes 49160 | tf_op jit(solution)/shard_map/ppermute | solution.py:310
  111.3 5.8 %collective-permute-start.21 = (f32[16,256]{1,0:T(8,128)S(1)}, f32[16,256]{1,0:T(8,128)S(1)}, u32[]{:S(2)}, u32[]{:S(2)}) collective-permute-start(f32[16,256]{1,0:T(8,128)S(1)} %add.107), channel_id=1, source_target_pairs={{0,192},{32,224},{64,128},{96,160},{128,64},{160,96},{192,0},{224,... | collective-permute-start | bytes 49160 | tf_op jit(solution)/shard_map/ppermute | solution.py:311
  114.9 3.7 %collective-permute-start.19 = (f32[16,256]{1,0:T(8,128)S(1)}, f32[16,256]{1,0:T(8,128)S(1)}, u32[]{:S(2)}, u32[]{:S(2)}) collective-permute-start(f32[16,256]{1,0:T(8,128)S(1)} %add.107), channel_id=1, source_target_pairs={{0,64},{32,96},{64,0},{96,32},{128,192},{160,224},{192,128},{224,1... | collective-permute-start | bytes 49160 | tf_op jit(solution)/shard_map/ppermute | solution.py:311
  117.0 6.7 %collective-permute-start.20 = (f32[16,256]{1,0:T(8,128)S(1)}, f32[16,256]{1,0:T(8,128)S(1)}, u32[]{:S(2)}, u32[]{:S(2)}) collective-permute-start(f32[16,256]{1,0:T(8,128)S(1)} %add.107), channel_id=1, source_target_pairs={{0,128},{32,160},{64,192},{96,224},{128,0},{160,32},{192,64},{224,... | collective-permute-start | bytes 49160 | tf_op jit(solution)/shard_map/ppermute | solution.py:311
  124.5 20.4 %all-to-all-start.2 = ((f32[32,16,256]{2,1,0:T(8,128)}), f32[32,16,256]{2,1,0:T(8,128)S(1)}, u32[]{:S(2)}, u32[]{:S(2)}) async-start(f32[32,16,256]{2,1,0:T(8,128)} %broadcast_in_dim.20), calls=%async_computation.2 | async-start | bytes 1048576 | tf_op jit(solution)/shard_map/all_to_all | solution.py:27
  145.0 26.8 %all-to-all-start.4 = ((bf16[256,8,128]{2,1,0:T(8,128)(2,1)}), bf16[256,8,128]{2,1,0:T(8,128)(2,1)S(1)}, u32[]{:S(2)}, u32[]{:S(2)}) async-start(bf16[256,8,128]{2,1,0:T(8,128)(2,1)} %bitcast.16), calls=%async_computation.4 | async-start | bytes 1048576 | tf_op jit(solution)/shard_map/all_to_all | solution.py:27
  (9 other events, 127.7 us)

commit v2 on v1

--- a/solution.py
+++ b/solution.py
@@ -11,7 +11,7 @@
 BLK = 256
 ROWS = 8 * BLK
 XK = ("x", "k")
-KYX = ("k", "y", "x")
+YX = ("y", "x")
 YZXK = ("y", "z", "x", "k")
 F32 = jnp.float32
 BF16 = jnp.bfloat16
@@ -67,18 +67,20 @@
     for b in range(8):
         scores = dot(items_ref[...], users_ref[b * BLK : (b + 1) * BLK, :], (1, 1))
         top = jnp.max(scores, axis=0, keepdims=True)
-        out_ref[0, pl.ds(at_ref[b], 1), :] = top
-        out_ref[0, pl.ds(8 + at_ref[b], 1), :] = jnp.sum(jnp.exp(scores - top), axis=0, keepdims=True)
-    out_ref[0, 16:40, :] = own_ref[...]
+        part = top + jnp.log(jnp.sum(jnp.exp(scores - top), axis=0, keepdims=True))
+        out_ref[0, pl.ds(at_ref[b], 1), :] = part
     for p in range(1, 8):
-        out_ref[p] = out_ref[0]
+        out_ref[p, :8, :] = out_ref[0, :8, :]
+    for p in range(8):
+        out_ref[p, 8:16, :] = own_ref[p]
 
 
 def stats(at, items, users, own):
     return pl.pallas_call(
         stats_kernel,
         in_specs=[SMEM, VMEM, VMEM, VMEM],
-        out_shape=jax.ShapeDtypeStruct((8, 40, BLK), F32),
+        out_specs=VMEM,
+        out_shape=jax.ShapeDtypeStruct((8, 16, BLK), F32),
         compiler_params=pltpu.CompilerParams(vmem_limit_bytes=20 * 2**20),
         name="stats",
     )(at, items, users, own)
@@ -93,12 +95,11 @@
     for b in range(8):
         c = at_ref[b]
         tops = got_ref[:, pl.ds(c, 1), :].reshape(8, BLK)
-        parts = got_ref[:, pl.ds(8 + c, 1), :].reshape(8, BLK)
-        own = got_ref[pl.ds(c, 1), 16:18, :].reshape(2, BLK)
+        own = got_ref[pl.ds(c, 1), 8:10, :].reshape(2, BLK)
         weight = own[0:1]
         target = own[1:2].astype(jnp.int32)
         top = jnp.max(tops, axis=0, keepdims=True)
-        total = top + jnp.log(jnp.sum(parts * jnp.exp(tops - top), axis=0, keepdims=True))
+        total = top + jnp.log(jnp.sum(jnp.exp(tops - top), axis=0, keepdims=True))
         total = total - jnp.log(weight)
         scores = dot(items_ref[...], users_ref[b * BLK : (b + 1) * BLK, :], (1, 1))
         share = jnp.exp(scores - total)
@@ -124,7 +125,7 @@
     )(at, items, users, got)
 
 
-def items_kernel(at_ref, all_ref, users_ref, got_ref, gi_ref, ids_ref):
+def items_kernel(all_ref, users_ref, got_ref, gi_ref, ids_ref):
     gi = dot(all_ref[...], users_ref[...], (1, 0))
     ids_ref[...] = jnp.zeros_like(ids_ref)
     for z in range(8):
@@ -135,26 +136,29 @@
         gi_ref[z, :BLK, :] = whole.astype(jnp.int32).astype(jnp.int16)
         ids_ref[z, 4:5, :] = power
     lane = lax.broadcasted_iota(jnp.int32, (8, 128), 1) // CAP
+    line = lax.broadcasted_iota(jnp.int32, (8, 128), 0)
     for y in range(4):
         row = jnp.zeros((8, 128), F32)
         for p in range(8):
-            piece = got_ref[p, 24 + 8 * (y // 2) : 32 + 8 * (y // 2), 128 * (y % 2) : 128 * (y % 2) + 128]
-            turn = ((p - at_ref[9]) & 7) * CAP
-            row = jnp.where(lane == p, pltpu.roll(piece, turn, 1), row)
+            piece = got_ref[p, 10 + y // 2 : 11 + y // 2, 128 * (y % 2) : 128 * (y % 2) + 128]
+            piece = jnp.broadcast_to(piece, (8, 128))
+            for z in range(8):
+                turn = (p - z) % 8 * CAP
+                row = jnp.where((lane == p) & (line == z), pltpu.roll(piece, turn, 1) if turn else piece, row)
         ids_ref[:, y, :128] = row
     gi_ref[:, BLK:, :] = ids_ref[...].astype(jnp.int32).astype(jnp.int16)
 
 
-def item_side(at, dscore, users, got):
+def item_side(dscore, users, got):
     return pl.pallas_call(
         items_kernel,
-        in_specs=[SMEM, VMEM, VMEM, VMEM],
+        in_specs=[VMEM, VMEM, VMEM],
         out_specs=VMEM,
         out_shape=jax.ShapeDtypeStruct((8, BLK + 8, 256), jnp.int16),
         scratch_shapes=[pltpu.VMEM((8, 8, 256), F32)],
         compiler_params=pltpu.CompilerParams(vmem_limit_bytes=22 * 2**20),
         name="item_side",
-    )(at, dscore, users, got)
+    )(dscore, users, got)
 
 
 def tower_kernel(
@@ -273,7 +277,7 @@
     block_no = jnp.arange(8, dtype=jnp.int32)
     source = 2 * ((lax.axis_index("x") - block_no // 2) & 3) + ((block_no % 2) ^ lax.axis_index("k"))
     own_place = lax.axis_index(XK).reshape(1)
-    at = jnp.concatenate([source, own_place * BLK, own_place]).astype(jnp.int32)
+    at = jnp.concatenate([source, own_place * BLK]).astype(jnp.int32)
 
     member = (owner == lax.broadcasted_iota(jnp.int32, (64, 1), 0)).astype(F32)
     order = lax.broadcasted_iota(jnp.int32, (BLK, BLK), 0) < lax.broadcasted_iota(jnp.int32, (BLK, BLK), 1)
@@ -283,14 +287,15 @@
     held = (slot == lax.broadcasted_iota(jnp.int32, (64 * CAP, 1), 0)).astype(jnp.int32)
     rows = jnp.sum(held * (item_row + 1), axis=1).astype(F32).reshape(64, CAP)
     rows = joined(rows, "y")
-    rows = rows.reshape(2, 2, 8, 128).swapaxes(1, 2).reshape(16, BLK)
+    rows = rows.reshape(4, 8, 8, CAP).transpose(2, 0, 1, 3).reshape(8, 2, BLK)
+    own = jnp.concatenate([example_weight, positive.astype(F32)], axis=0)
     own = jnp.concatenate(
-        [example_weight, positive.astype(F32), jnp.zeros((6, BLK), F32), rows], axis=0
+        [jnp.broadcast_to(own[None], (8, 2, BLK)), rows, jnp.zeros((8, 4, BLK), F32)], axis=1
     )
     got = exchange(stats(at, items, users, own), XK)
     dscore, keep, give = user_side(at, items, users, got)
     swapped = shifted(give, "k", 1)
-    gi = item_side(at, dscore, users, got)
+    gi = item_side(dscore, users, got)
     gi = exchange(gi, "z")
     gu = keep + swapped
     parts = [gu] + [shifted(gu[d], "x", -d) for d in range(1, 4)]
@@ -312,9 +317,11 @@
 
     send = pack(gi, owner, rank).reshape(256, 8, 128)
     came = exchange(send, YZXK).reshape(256 * 8, 128)
-    both = to_all(both, KYX).reshape(512, 256)
+    both = to_all(both, YX).reshape(256, 256)
     grad_table = table(came, ids).T
-    return both[:256], both[256:], grad_table
+    other = shifted(both, "k", 1)
+    first = lax.axis_index("k") == 0
+    return jnp.where(first, both, other), jnp.where(first, other, both), grad_table
 
 
 def solution(mesh):

time: 177 us -> 176 us (level)
  blocking collectives: 12.1 us -> 9.82 us
  other arithmetic: 1.85 us -> 4.12 us
    all_to_all x4, waiting for transfers between devices: 33.1 us -> 28.9 us  [exchange(): return lax.all_to_all(value, axes, 0, 0, tiled=True)]
    ppermute x18 -> x19, starting transfers between devices: 19.1 us -> 23.2 us  [shifted(): lax.ppermute(value, axis, [(i, (i + step) % count) for i in range(count)])]
    ppermute x18 -> x19, waiting for transfers between devices: 31.1 us -> 34.3 us  [shifted(): lax.ppermute(value, axis, [(i, (i + step) % count) for i in range(count)])]
    all_to_all x1, blocking collectives: 12.1 us -> 9.82 us  [exchange(): return lax.all_to_all(value, axes, 0, 0, tiled=True)]
    all_to_all x4, starting transfers between devices: 29.2 us -> 27.1 us  [exchange(): return lax.all_to_all(value, axes, 0, 0, tiled=True)]
  transfers between devices with their start and end apart: 26 -> 27, of which waited for: 20 -> 19; matrix products, arithmetic and copies ran while one was open for 5% -> 6% of each run, Pallas kernels for 4% -> 3%
where the time goes in v2:
time: 176 us
  waiting for transfers between devices  71 us (40%)
  starting transfers between devices  57.4 us (33%)
  Pallas kernels  22.4 us (13%)
  blocking collectives  9.82 us (6%)
  local copies, waits for them, and re-layouts  7.03 us (4%)
  other arithmetic  4.12 us (2%)
  matrix products  2.98 us (2%)
    ppermute x19, waiting for transfers between devices, shifted(): lax.ppermute(value, axis, [(i, (i + step) % count) for i in range(count)])  34.3 us
    all_to_all x4, waiting for transfers between devices, exchange(): return lax.all_to_all(value, axes, 0, 0, tiled=True)  28.9 us
    all_to_all x4, starting transfers between devices, exchange(): return lax.all_to_all(value, axes, 0, 0, tiled=True)  27.1 us
    ppermute x19, starting transfers between devices, shifted(): lax.ppermute(value, axis, [(i, (i + step) % count) for i in range(count)])  23.2 us
    all_to_all x1, blocking collectives, exchange(): return lax.all_to_all(value, axes, 0, 0, tiled=True)  9.82 us
    pallas_call x1, Pallas kernels, user_side(): pl.pallas_call(users_kernel, in_specs=[SMEM, VMEM, VMEM, VMEM], out_specs...  6.61 us
    ppermute x3, waiting for transfers between devices, step_body(): lax.ppermute(both, 'z', [(i, i ^ step) for i in range(8)])  6.57 us
    ppermute x3, starting transfers between devices, step_body(): lax.ppermute(both, 'z', [(i, i ^ step) for i in range(8)])  5.67 us
  transfers between devices with their start and end apart: 27, of which 19 were waited for; matrix products, arithmetic and copies ran while one was open for 6% of the time, Pallas kernels for 3%

profile of v2, /device:TPU:1, one launch (start us, length us, event | category | flops | bytes accessed | tf_op | source)
XLA Modules:
  0.0 175.7 jit_solution(2445498631286285997)
XLA Ops:
  3.3 3.6 %collective-permute-start.4 = (f32[64,16]{1,0:T(8,128)S(1)}, f32[64,16]{1,0:T(8,128)S(1)}, u32[]{:S(2)}, u32[]{:S(2)}) collective-permute-start(f32[64,16]{1,0:T(8,128)S(1)} %convert_element_type.52), channel_id=1, source_target_pairs={{0,3},{1,0},{2,1},{3,2},{4,7},{5,4},{6,5},{7,6},{8,11},{9,8},{10,9... | collective-permute-start | bytes 12296 | tf_op jit(solution)/shard_map/ppermute | solution.py:36
  9.9 8.2 %all-to-all-start = ((bf16[8,256,256]{2,1,0:T(8,128)(2,1)}), bf16[8,256,256]{2,1,0:T(8,128)(2,1)S(1)}, u32[]{:S(2)}, u32[]{:S(2)}) async-start(bf16[8,256,256]{2,1,0:T(8,128)(2,1)} %broadcast_in_dim.11), calls=%async_computation | async-start | bytes 2097152 | tf_op jit(solution)/shard_map/all_to_all | solution.py:27
  22.5 2.5 %collective-permute-start.2 = (bf16[512,256]{1,0:T(8,128)(2,1)S(1)}, bf16[512,256]{1,0:T(8,128)(2,1)S(1)}, u32[]{:S(2)}, u32[]{:S(2)}) collective-permute-start(bf16[512,256]{1,0:T(8,128)(2,1)S(1)} %pad_maximum_fusion), channel_id=1, source_target_pairs={{0,16},{8,24},{16,0},{24,8},{1,17},{9,25},{17,1},{25,9},{2,18},{10... | collective-permute-start | bytes 786440 | tf_op jit(solution)/shard_map/ppermute | solution.py:36
  26.8 3.3 %collective-permute-done.1 = bf16[512,256]{1,0:T(8,128)(2,1)S(1)} collective-permute-done((bf16[512,256]{1,0:T(8,128)(2,1)S(1)}, bf16[512,256]{1,0:T(8,128)(2,1)S(1)}, u32[]{:S(2)}, u32[]{:S(2)}) %collective-permute-start.1) | collective-permute-done | bytes 262176 | tf_op jit(solution)/shard_map/ppermute | solution.py:36
  30.9 5.9 %collective-permute-done.2 = bf16[512,256]{1,0:T(8,128)(2,1)S(1)} collective-permute-done((bf16[512,256]{1,0:T(8,128)(2,1)S(1)}, bf16[512,256]{1,0:T(8,128)(2,1)S(1)}, u32[]{:S(2)}, u32[]{:S(2)}) %collective-permute-start.2) | collective-permute-done | bytes 262176 | tf_op jit(solution)/shard_map/ppermute | solution.py:36
  40.3 7.0 %all-to-all-done = bf16[8,256,256]{2,1,0:T(8,128)(2,1)S(1)} async-done(((bf16[8,256,256]{2,1,0:T(8,128)(2,1)}), bf16[8,256,256]{2,1,0:T(8,128)(2,1)S(1)}, u32[]{:S(2)}, u32[]{:S(2)}) %all-to-all-start) | async-done | bytes 1048608 | tf_op jit(solution)/shard_map/all_to_all | solution.py:27
  47.3 5.2 %stats.1 = f32[8,16,256]{2,1,0:T(8,128)S(1)} custom-call(s32[9]{0:T(128)S(1)} %pad_add_fusion.1.at_ref, bf16[2048,256]{1,0:T(8,128)(2,1)S(1)} %bitcast.32, bf16[2048,256]{1,0:T(8,128)(2,1)S(1)} %convolution_convert_fusion.users_ref, f32[8,8,256]{2,1,0:T(8,128)S(1)} %maximum_maximum_fusion.own_ref), custom_call_target="tpu_custom_call" | custom-call | tf_op jit(solution)/shard_map/stats/pallas_call | solution.py:79
  52.4 9.8 %all_to_all.25.got_ref = f32[8,16,256]{2,1,0:T(8,128)S(1)} all-to-all(f32[8,16,256]{2,1,0:T(8,128)S(1)} %stats.1), channel_id=1, replica_groups=mesh['z'=8,'x'=4,'k'=2,'y'=4] {'x','k'}, dimensions={0} | all-to-all | bytes 262144 | tf_op jit(solution)/shard_map/all_to_all | solution.py:27
  62.2 6.6 %user_side.1 = (bf16[2048,2048]{1,0:T(8,128)(2,1)S(1)}, f32[4,256,256]{2,1,0:T(8,128)S(1)}, f32[4,256,256]{2,1,0:T(8,128)}) custom-call(s32[9]{0:T(128)S(1)} %pad_add_fusion.1.at_ref, bf16[2048,256]{1,0:T(8,128)(2,1)S(1)} %bitcast.33, bf16[2048,256]{1,0:T(8,128)(2,1)S(1)} %convolution_convert_fusion.users_ref, f32[8,16,256]{2,1,0:T(8,128)S(1)} %all_to_all.25.got_ref), custom_call_target="tpu_custom_call" | custom-call | tf_op jit(solution)/shard_map/user_side/pallas_call | solution.py:117
  69.7 4.0 %item_side.1 = s16[8,264,256]{2,1,0:T(8,128)(2,1)} custom-call(bf16[2048,2048]{1,0:T(8,128)(2,1)S(1)} %get-tuple-element.12.all_ref, bf16[2048,256]{1,0:T(8,128)(2,1)S(1)} %convolution_convert_fusion.users_ref, f32[8,16,256]{2,1,0:T(8,128)S(1)} %all_to_all.25.got_ref), custom_call_target="tpu_custom_call" | custom-call | tf_op jit(solution)/shard_map/item_side/pallas_call | solution.py:153
  73.8 3.6 %all-to-all-start.3 = ((s16[8,264,256]{2,1,0:T(8,128)(2,1)}), s16[8,264,256]{2,1,0:T(8,128)(2,1)S(1)}, u32[]{:S(2)}, u32[]{:S(2)}) async-start(s16[8,264,256]{2,1,0:T(8,128)(2,1)} %item_side.1), calls=%async_computation.3 | async-start | bytes 2162688 | tf_op jit(solution)/shard_map/all_to_all | solution.py:27
  80.9 5.8 %collective-permute-done.8.one_ref = f32[256,256]{1,0:T(8,128)S(1)} collective-permute-done((f32[256,256]{1,0:T(8,128)S(1)}, f32[256,256]{1,0:T(8,128)S(1)}, u32[]{:S(2)}, u32[]{:S(2)}) %collective-permute-start.8) | collective-permute-done | bytes 262176 | tf_op jit(solution)/shard_map/ppermute | solution.py:36
  86.7 2.2 %collective-permute-done.9.two_ref = f32[256,256]{1,0:T(8,128)S(1)} collective-permute-done((f32[256,256]{1,0:T(8,128)S(1)}, f32[256,256]{1,0:T(8,128)S(1)}, u32[]{:S(2)}, u32[]{:S(2)}) %collective-permute-start.9) | collective-permute-done | bytes 262176 | tf_op jit(solution)/shard_map/ppermute | solution.py:36
  88.9 6.2 %collective-permute-done.10.three_ref = f32[256,256]{1,0:T(8,128)S(1)} collective-permute-done((f32[256,256]{1,0:T(8,128)S(1)}, f32[256,256]{1,0:T(8,128)S(1)}, u32[]{:S(2)}, u32[]{:S(2)}) %collective-permute-start.10) | collective-permute-done | bytes 262176 | tf_op jit(solution)/shard_map/ppermute | solution.py:36
  97.5 2.3 %collective-permute-start.14 = (f32[64,256]{1,0:T(8,128)S(1)}, f32[64,256]{1,0:T(8,128)S(1)}, u32[]{:S(2)}, u32[]{:S(2)}) collective-permute-start(f32[64,256]{1,0:T(8,128)S(1)} %get-tuple-element.19), channel_id=1, source_target_pairs={{0,3},{1,0},{2,1},{3,2},{4,7},{5,4},{6,5},{7,6},{8,11},{9,8},{10,9... | collective-permute-start | bytes 196616 | tf_op jit(solution)/shard_map/ppermute | solution.py:36
  101.4 3.3 %collective-permute-done.13 = f32[64,256]{1,0:T(8,128)S(1)} collective-permute-done((f32[64,256]{1,0:T(8,128)S(1)}, f32[64,256]{1,0:T(8,128)S(1)}, u32[]{:S(2)}, u32[]{:S(2)}) %collective-permute-start.13) | collective-permute-done | bytes 65568 | tf_op jit(solution)/shard_map/ppermute | solution.py:36
  114.6 3.5 %collective-permute-start.21 = (f32[16,256]{1,0:T(8,128)S(1)}, f32[16,256]{1,0:T(8,128)S(1)}, u32[]{:S(2)}, u32[]{:S(2)}) collective-permute-start(f32[16,256]{1,0:T(8,128)S(1)} %add.107), channel_id=1, source_target_pairs={{0,192},{32,224},{64,128},{96,160},{128,64},{160,96},{192,0},{224,... | collective-permute-start | bytes 49160 | tf_op jit(solution)/shard_map/ppermute | solution.py:316
  121.8 5.1 %collective-permute-done.20 = f32[16,256]{1,0:T(8,128)S(1)} collective-permute-done((f32[16,256]{1,0:T(8,128)S(1)}, f32[16,256]{1,0:T(8,128)S(1)}, u32[]{:S(2)}, u32[]{:S(2)}) %collective-permute-start.20) | collective-permute-done | bytes 16416 | tf_op jit(solution)/shard_map/ppermute | solution.py:316
  127.6 3.8 %all-to-all-start.2 = ((f32[16,16,256]{2,1,0:T(8,128)}), f32[16,16,256]{2,1,0:T(8,128)S(1)}, u32[]{:S(2)}, u32[]{:S(2)}) async-start(f32[16,16,256]{2,1,0:T(8,128)} %broadcast_in_dim.27), calls=%async_computation.2 | async-start | bytes 524288 | tf_op jit(solution)/shard_map/all_to_all | solution.py:27
  132.8 6.1 %all-to-all-done.2 = f32[16,16,256]{2,1,0:T(8,128)S(1)} async-done(((f32[16,16,256]{2,1,0:T(8,128)}), f32[16,16,256]{2,1,0:T(8,128)S(1)}, u32[]{:S(2)}, u32[]{:S(2)}) %all-to-all-start.2) | async-done | bytes 262176 | tf_op jit(solution)/shard_map/all_to_all | solution.py:27
  138.9 11.6 %all-to-all-start.4 = ((bf16[256,8,128]{2,1,0:T(8,128)(2,1)}), bf16[256,8,128]{2,1,0:T(8,128)(2,1)S(1)}, u32[]{:S(2)}, u32[]{:S(2)}) async-start(bf16[256,8,128]{2,1,0:T(8,128)(2,1)} %bitcast.15), calls=%async_computation.4 | async-start | bytes 1048576 | tf_op jit(solution)/shard_map/all_to_all | solution.py:27
  151.0 2.4 %collective-permute-start.22 = (f32[256,256]{1,0:T(8,128)S(1)}, f32[256,256]{1,0:T(8,128)S(1)}, u32[]{:S(2)}, u32[]{:S(2)}) collective-permute-start(f32[256,256]{1,0:T(8,128)S(1)} %bitcast.43), channel_id=1, source_target_pairs={{0,4},{4,0},{1,5},{5,1},{2,6},{6,2},{3,7},{7,3},{8,12},{12,8},{9,1... | collective-permute-start | bytes 786440 | tf_op jit(solution)/shard_map/ppermute | solution.py:36
  155.3 15.8 %all-to-all-done.4 = bf16[256,8,128]{2,1,0:T(8,128)(2,1)S(1)} async-done(((bf16[256,8,128]{2,1,0:T(8,128)(2,1)}), bf16[256,8,128]{2,1,0:T(8,128)(2,1)S(1)}, u32[]{:S(2)}, u32[]{:S(2)}) %all-to-all-start.4) | async-done | bytes 524320 | tf_op jit(solution)/shard_map/all_to_all | solution.py:27
  171.1 4.6 %table.1 = f32[64,4096]{1,0:T(8,128)} custom-call(bf16[2048,128]{1,0:T(8,128)(2,1)S(1)} %bitcast.34, s32[1,4096]{1,0:T(1,128)S(1)} %pad_add_fusion.ids_ref), custom_call_target="tpu_custom_call" | custom-call | tf_op jit(solution)/shard_map/table/pallas_call | solution.py:252
  (101 shorter events, 42.6 us)
Async XLA Ops:
  3.3 17.5 %collective-permute-start.4 = (f32[64,16]{1,0:T(8,128)S(1)}, f32[64,16]{1,0:T(8,128)S(1)}, u32[]{:S(2)}, u32[]{:S(2)}) collective-permute-start(f32[64,16]{1,0:T(8,128)S(1)} %convert_element_type.52), channel_id=1, source_target_pairs={{0,3},{1,0},{2,1},{3,2},{4,7},{5,4},{6,5},{7,6},{8,11},{9,8},{10,9... | collective-permute-start | bytes 12296 | tf_op jit(solution)/shard_map/ppermute | solution.py:36
  6.9 14.0 %collective-permute-start.5 = (f32[64,16]{1,0:T(8,128)S(1)}, f32[64,16]{1,0:T(8,128)S(1)}, u32[]{:S(2)}, u32[]{:S(2)}) collective-permute-start(f32[64,16]{1,0:T(8,128)S(1)} %convert_element_type.52), channel_id=1, source_target_pairs={{0,2},{1,3},{2,0},{3,1},{4,6},{5,7},{6,4},{7,5},{8,10},{9,11},{10,... | collective-permute-start | bytes 12296 | tf_op jit(solution)/shard_map/ppermute | solution.py:36
  7.3 13.6 %collective-permute-start.6 = (f32[64,16]{1,0:T(8,128)S(1)}, f32[64,16]{1,0:T(8,128)S(1)}, u32[]{:S(2)}, u32[]{:S(2)}) collective-permute-start(f32[64,16]{1,0:T(8,128)S(1)} %convert_element_type.52), channel_id=1, source_target_pairs={{0,1},{1,2},{2,3},{3,0},{4,5},{5,6},{6,7},{7,4},{8,9},{9,10},{10,1... | collective-permute-start | bytes 12296 | tf_op jit(solution)/shard_map/ppermute | solution.py:36
  9.9 37.4 %all-to-all-start = ((bf16[8,256,256]{2,1,0:T(8,128)(2,1)}), bf16[8,256,256]{2,1,0:T(8,128)(2,1)S(1)}, u32[]{:S(2)}, u32[]{:S(2)}) async-start(bf16[8,256,256]{2,1,0:T(8,128)(2,1)} %broadcast_in_dim.11), calls=%async_computation | async-start | bytes 2097152 | tf_op jit(solution)/shard_map/all_to_all | solution.py:27
  18.1 3.0 %collective-permute-start = (bf16[256,256]{1,0:T(8,128)(2,1)S(1)}, bf16[256,256]{1,0:T(8,128)(2,1)S(1)}, u32[]{:S(2)}, u32[]{:S(2)}) collective-permute-start(bf16[256,256]{1,0:T(8,128)(2,1)S(1)} %bitcast.35), channel_id=1, source_target_pairs={{0,4},{4,0},{1,5},{5,1},{2,6},{6,2},{3,7},{7,3},{8,12},{12,8},{9,1... | collective-permute-start | bytes 393224 | tf_op jit(solution)/shard_map/ppermute | solution.py:36
  21.2 9.0 %collective-permute-start.1 = (bf16[512,256]{1,0:T(8,128)(2,1)S(1)}, bf16[512,256]{1,0:T(8,128)(2,1)S(1)}, u32[]{:S(2)}, u32[]{:S(2)}) collective-permute-start(bf16[512,256]{1,0:T(8,128)(2,1)S(1)} %pad_maximum_fusion), channel_id=1, source_target_pairs={{0,8},{8,16},{16,24},{24,0},{1,9},{9,17},{17,25},{25,1},{2,10},{10... | collective-permute-start | bytes 786440 | tf_op jit(solution)/shard_map/ppermute | solution.py:36
  22.5 14.3 %collective-permute-start.2 = (bf16[512,256]{1,0:T(8,128)(2,1)S(1)}, bf16[512,256]{1,0:T(8,128)(2,1)S(1)}, u32[]{:S(2)}, u32[]{:S(2)}) collective-permute-start(bf16[512,256]{1,0:T(8,128)(2,1)S(1)} %pad_maximum_fusion), channel_id=1, source_target_pairs={{0,16},{8,24},{16,0},{24,8},{1,17},{9,25},{17,1},{25,9},{2,18},{10... | collective-permute-start | bytes 786440 | tf_op jit(solution)/shard_map/ppermute | solution.py:36
  25.0 12.5 %collective-permute-start.3 = (bf16[512,256]{1,0:T(8,128)(2,1)S(1)}, bf16[512,256]{1,0:T(8,128)(2,1)S(1)}, u32[]{:S(2)}, u32[]{:S(2)}) collective-permute-start(bf16[512,256]{1,0:T(8,128)(2,1)S(1)} %pad_maximum_fusion), channel_id=1, source_target_pairs={{0,24},{8,0},{16,8},{24,16},{1,25},{9,1},{17,9},{25,17},{2,26},{10... | collective-permute-start | bytes 786440 | tf_op jit(solution)/shard_map/ppermute | solution.py:36
  68.9 8.5 %collective-permute-start.7 = (f32[4,256,256]{2,1,0:T(8,128)}, f32[4,256,256]{2,1,0:T(8,128)}, u32[]{:S(2)}, u32[]{:S(2)}) collective-permute-start(f32[4,256,256]{2,1,0:T(8,128)} %get-tuple-element.9), channel_id=1, source_target_pairs={{0,4},{4,0},{1,5},{5,1},{2,6},{6,2},{3,7},{7,3},{8,12},{12,8},{9,1... | collective-permute-start | bytes 3145736 | tf_op jit(solution)/shard_map/ppermute | solution.py:36
  73.8 53.1 %all-to-all-start.3 = ((s16[8,264,256]{2,1,0:T(8,128)(2,1)}), s16[8,264,256]{2,1,0:T(8,128)(2,1)S(1)}, u32[]{:S(2)}, u32[]{:S(2)}) async-start(s16[8,264,256]{2,1,0:T(8,128)(2,1)} %item_side.1), calls=%async_computation.3 | async-start | bytes 2162688 | tf_op jit(solution)/shard_map/all_to_all | solution.py:27
  78.8 7.9 %collective-permute-start.8 = (f32[256,256]{1,0:T(8,128)S(1)}, f32[256,256]{1,0:T(8,128)S(1)}, u32[]{:S(2)}, u32[]{:S(2)}) collective-permute-start(f32[256,256]{1,0:T(8,128)S(1)} %get-tuple-element.15), channel_id=1, source_target_pairs={{0,24},{8,0},{16,8},{24,16},{1,25},{9,1},{17,9},{25,17},{2,26},{10... | collective-permute-start | bytes 786440 | tf_op jit(solution)/shard_map/ppermute | solution.py:36
  79.7 9.1 %collective-permute-start.9 = (f32[256,256]{1,0:T(8,128)S(1)}, f32[256,256]{1,0:T(8,128)S(1)}, u32[]{:S(2)}, u32[]{:S(2)}) collective-permute-start(f32[256,256]{1,0:T(8,128)S(1)} %get-tuple-element.14), channel_id=1, source_target_pairs={{0,16},{8,24},{16,0},{24,8},{1,17},{9,25},{17,1},{25,9},{2,18},{10... | collective-permute-start | bytes 786440 | tf_op jit(solution)/shard_map/ppermute | solution.py:36
  80.9 14.2 %collective-permute-start.10 = (f32[256,256]{1,0:T(8,128)S(1)}, f32[256,256]{1,0:T(8,128)S(1)}, u32[]{:S(2)}, u32[]{:S(2)}) collective-permute-start(f32[256,256]{1,0:T(8,128)S(1)} %get-tuple-element.13), channel_id=1, source_target_pairs={{0,8},{8,16},{16,24},{24,0},{1,9},{9,17},{17,25},{25,1},{2,10},{10... | collective-permute-start | bytes 786440 | tf_op jit(solution)/shard_map/ppermute | solution.py:36
  97.5 3.9 %collective-permute-start.14 = (f32[64,256]{1,0:T(8,128)S(1)}, f32[64,256]{1,0:T(8,128)S(1)}, u32[]{:S(2)}, u32[]{:S(2)}) collective-permute-start(f32[64,256]{1,0:T(8,128)S(1)} %get-tuple-element.19), channel_id=1, source_target_pairs={{0,3},{1,0},{2,1},{3,2},{4,7},{5,4},{6,5},{7,6},{8,11},{9,8},{10,9... | collective-permute-start | bytes 196616 | tf_op jit(solution)/shard_map/ppermute | solution.py:36
  99.8 4.9 %collective-permute-start.13 = (f32[64,256]{1,0:T(8,128)S(1)}, f32[64,256]{1,0:T(8,128)S(1)}, u32[]{:S(2)}, u32[]{:S(2)}) collective-permute-start(f32[64,256]{1,0:T(8,128)S(1)} %get-tuple-element.20), channel_id=1, source_target_pairs={{0,2},{1,3},{2,0},{3,1},{4,6},{5,7},{6,4},{7,5},{8,10},{9,11},{10,... | collective-permute-start | bytes 196616 | tf_op jit(solution)/shard_map/ppermute | solution.py:36
  101.2 5.3 %collective-permute-start.12 = (f32[64,256]{1,0:T(8,128)S(1)}, f32[64,256]{1,0:T(8,128)S(1)}, u32[]{:S(2)}, u32[]{:S(2)}) collective-permute-start(f32[64,256]{1,0:T(8,128)S(1)} %get-tuple-element.18), channel_id=1, source_target_pairs={{0,1},{1,2},{2,3},{3,0},{4,5},{5,6},{6,7},{7,4},{8,9},{9,10},{10,1... | collective-permute-start | bytes 196616 | tf_op jit(solution)/shard_map/ppermute | solution.py:36
  106.9 4.1 %collective-permute-start.16 = (f32[16,256]{1,0:T(8,128)S(1)}, f32[16,256]{1,0:T(8,128)S(1)}, u32[]{:S(2)}, u32[]{:S(2)}) collective-permute-start(f32[16,256]{1,0:T(8,128)S(1)} %get-tuple-element.25), channel_id=1, source_target_pairs={{0,16},{8,24},{16,0},{24,8},{1,17},{9,25},{17,1},{25,9},{2,18},{10... | collective-permute-start | bytes 49160 | tf_op jit(solution)/shard_map/ppermute | solution.py:36
  108.1 3.8 %collective-permute-start.15 = (f32[16,256]{1,0:T(8,128)S(1)}, f32[16,256]{1,0:T(8,128)S(1)}, u32[]{:S(2)}, u32[]{:S(2)}) collective-permute-start(f32[16,256]{1,0:T(8,128)S(1)} %get-tuple-element.23), channel_id=1, source_target_pairs={{0,8},{8,16},{16,24},{24,0},{1,9},{9,17},{17,25},{25,1},{2,10},{10... | collective-permute-start | bytes 49160 | tf_op jit(solution)/shard_map/ppermute | solution.py:36
  114.6 5.7 %collective-permute-start.21 = (f32[16,256]{1,0:T(8,128)S(1)}, f32[16,256]{1,0:T(8,128)S(1)}, u32[]{:S(2)}, u32[]{:S(2)}) collective-permute-start(f32[16,256]{1,0:T(8,128)S(1)} %add.107), channel_id=1, source_target_pairs={{0,192},{32,224},{64,128},{96,160},{128,64},{160,96},{192,0},{224,... | collective-permute-start | bytes 49160 | tf_op jit(solution)/shard_map/ppermute | solution.py:316
  118.1 3.7 %collective-permute-start.19 = (f32[16,256]{1,0:T(8,128)S(1)}, f32[16,256]{1,0:T(8,128)S(1)}, u32[]{:S(2)}, u32[]{:S(2)}) collective-permute-start(f32[16,256]{1,0:T(8,128)S(1)} %add.107), channel_id=1, source_target_pairs={{0,64},{32,96},{64,0},{96,32},{128,192},{160,224},{192,128},{224,1... | collective-permute-start | bytes 49160 | tf_op jit(solution)/shard_map/ppermute | solution.py:316
  120.2 6.7 %collective-permute-start.20 = (f32[16,256]{1,0:T(8,128)S(1)}, f32[16,256]{1,0:T(8,128)S(1)}, u32[]{:S(2)}, u32[]{:S(2)}) collective-permute-start(f32[16,256]{1,0:T(8,128)S(1)} %add.107), channel_id=1, source_target_pairs={{0,128},{32,160},{64,192},{96,224},{128,0},{160,32},{192,64},{224,... | collective-permute-start | bytes 49160 | tf_op jit(solution)/shard_map/ppermute | solution.py:316
  127.6 11.3 %all-to-all-start.2 = ((f32[16,16,256]{2,1,0:T(8,128)}), f32[16,16,256]{2,1,0:T(8,128)S(1)}, u32[]{:S(2)}, u32[]{:S(2)}) async-start(f32[16,16,256]{2,1,0:T(8,128)} %broadcast_in_dim.27), calls=%async_computation.2 | async-start | bytes 524288 | tf_op jit(solution)/shard_map/all_to_all | solution.py:27
  138.9 32.2 %all-to-all-start.4 = ((bf16[256,8,128]{2,1,0:T(8,128)(2,1)}), bf16[256,8,128]{2,1,0:T(8,128)(2,1)S(1)}, u32[]{:S(2)}, u32[]{:S(2)}) async-start(bf16[256,8,128]{2,1,0:T(8,128)(2,1)} %bitcast.15), calls=%async_computation.4 | async-start | bytes 1048576 | tf_op jit(solution)/shard_map/all_to_all | solution.py:27
  151.0 3.5 %collective-permute-start.22 = (f32[256,256]{1,0:T(8,128)S(1)}, f32[256,256]{1,0:T(8,128)S(1)}, u32[]{:S(2)}, u32[]{:S(2)}) collective-permute-start(f32[256,256]{1,0:T(8,128)S(1)} %bitcast.43), channel_id=1, source_target_pairs={{0,4},{4,0},{1,5},{5,1},{2,6},{6,2},{3,7},{7,3},{8,12},{12,8},{9,1... | collective-permute-start | bytes 786440 | tf_op jit(solution)/shard_map/ppermute | solution.py:36
  (9 other events, 141.2 us)

commit v3 on v2

--- a/solution.py
+++ b/solution.py
@@ -312,8 +312,8 @@
     both = both + shifted(other, "k", 1)
     both = summed_share(both, "y")
     both = summed_share(both, "x")
-    both = both + lax.ppermute(both, "z", [(i, i ^ 1) for i in range(8)])
-    both = both + sum(lax.ppermute(both, "z", [(i, i ^ step) for i in range(8)]) for step in (2, 4, 6))
+    for step in (1, 2, 4):
+        both = both + lax.ppermute(both, "z", [(i, i ^ step) for i in range(8)])
 
     send = pack(gi, owner, rank).reshape(256, 8, 128)
     came = exchange(send, YZXK).reshape(256 * 8, 128)
@@ -337,4 +337,6 @@
         P("y", rows, None),
         P("y", rows),
     )
-    return jax.shard_map(step_body, mesh=torus, in_specs=placed, out_specs=(P(), P(), P(rows, "y")), check_vma=False)
+    return jax.shard_map(
+        step_body, mesh=torus, in_specs=placed, out_specs=(P(), P(), P(rows, "y")), check_vma=False
+    )

time: 176 us -> 178 us (1.011)
  starting transfers between devices: 57.4 us -> 63.7 us
  waiting for transfers between devices: 71 us -> 66.8 us
    all_to_all x4, starting transfers between devices: 27.1 us -> 31.5 us  [exchange(): return lax.all_to_all(value, axes, 0, 0, tiled=True)]
    ppermute x4 -> x3, waiting for transfers between devices: 7.8 us -> 3.6 us  [step_body(): both = both + lax.ppermute(both, 'z', [(i, i ^ step) for i in range(8)])]
    ppermute x4 -> x3, starting transfers between devices: 7.11 us -> 9.15 us  [step_body(): both = both + lax.ppermute(both, 'z', [(i, i ^ step) for i in range(8)])]
  transfers between devices with their start and end apart: 27 -> 26, of which waited for: 19 -> 19; matrix products, arithmetic and copies ran while one was open for 6% -> 6% of each run, Pallas kernels for 3% -> 3%
where the time goes in v3:
time: 178 us
  waiting for transfers between devices  66.8 us (38%)
  starting transfers between devices  63.7 us (36%)
  Pallas kernels  22.4 us (13%)
  blocking collectives  9.82 us (6%)
  local copies, waits for them, and re-layouts  7.01 us (4%)
  other arithmetic  4.12 us (2%)
  matrix products  2.98 us (2%)
    ppermute x19, waiting for transfers between devices, shifted(): lax.ppermute(value, axis, [(i, (i + step) % count) for i in range(count)])  34.3 us
    all_to_all x4, starting transfers between devices, exchange(): return lax.all_to_all(value, axes, 0, 0, tiled=True)  31.5 us
    all_to_all x4, waiting for transfers between devices, exchange(): return lax.all_to_all(value, axes, 0, 0, tiled=True)  28.9 us
    ppermute x19, starting transfers between devices, shifted(): lax.ppermute(value, axis, [(i, (i + step) % count) for i in range(count)])  23.1 us
    all_to_all x1, blocking collectives, exchange(): return lax.all_to_all(value, axes, 0, 0, tiled=True)  9.82 us
    ppermute x3, starting transfers between devices, step_body(): both = both + lax.ppermute(both, 'z', [(i, i ^ step) for i in range(8)])  9.15 us
    pallas_call x1, Pallas kernels, user_side(): pl.pallas_call(users_kernel, in_specs=[SMEM, VMEM, VMEM, VMEM], out_specs...  6.61 us
    pallas_call x1, Pallas kernels, stats(): pl.pallas_call(stats_kernel, in_specs=[SMEM, VMEM, VMEM, VMEM], out_specs...  5.16 us
  transfers between devices with their start and end apart: 26, of which 19 were waited for; matrix products, arithmetic and copies ran while one was open for 6% of the time, Pallas kernels for 3%

profile of v3, /device:TPU:1, one launch (start us, length us, event | category | flops | bytes accessed | tf_op | source)
XLA Modules:
  0.0 177.8 jit_solution(13032220601667034561)
XLA Ops:
  3.3 3.6 %collective-permute-start.4 = (f32[64,16]{1,0:T(8,128)S(1)}, f32[64,16]{1,0:T(8,128)S(1)}, u32[]{:S(2)}, u32[]{:S(2)}) collective-permute-start(f32[64,16]{1,0:T(8,128)S(1)} %convert_element_type.52), channel_id=1, source_target_pairs={{0,3},{1,0},{2,1},{3,2},{4,7},{5,4},{6,5},{7,6},{8,11},{9,8},{10,9... | collective-permute-start | bytes 12296 | tf_op jit(solution)/shard_map/ppermute | solution.py:36
  9.9 8.2 %all-to-all-start = ((bf16[8,256,256]{2,1,0:T(8,128)(2,1)}), bf16[8,256,256]{2,1,0:T(8,128)(2,1)S(1)}, u32[]{:S(2)}, u32[]{:S(2)}) async-start(bf16[8,256,256]{2,1,0:T(8,128)(2,1)} %broadcast_in_dim.11), calls=%async_computation | async-start | bytes 2097152 | tf_op jit(solution)/shard_map/all_to_all | solution.py:27
  22.5 2.5 %collective-permute-start.2 = (bf16[512,256]{1,0:T(8,128)(2,1)S(1)}, bf16[512,256]{1,0:T(8,128)(2,1)S(1)}, u32[]{:S(2)}, u32[]{:S(2)}) collective-permute-start(bf16[512,256]{1,0:T(8,128)(2,1)S(1)} %pad_maximum_fusion), channel_id=1, source_target_pairs={{0,16},{8,24},{16,0},{24,8},{1,17},{9,25},{17,1},{25,9},{2,18},{10... | collective-permute-start | bytes 786440 | tf_op jit(solution)/shard_map/ppermute | solution.py:36
  26.8 3.3 %collective-permute-done.1 = bf16[512,256]{1,0:T(8,128)(2,1)S(1)} collective-permute-done((bf16[512,256]{1,0:T(8,128)(2,1)S(1)}, bf16[512,256]{1,0:T(8,128)(2,1)S(1)}, u32[]{:S(2)}, u32[]{:S(2)}) %collective-permute-start.1) | collective-permute-done | bytes 262176 | tf_op jit(solution)/shard_map/ppermute | solution.py:36
  30.9 5.9 %collective-permute-done.2 = bf16[512,256]{1,0:T(8,128)(2,1)S(1)} collective-permute-done((bf16[512,256]{1,0:T(8,128)(2,1)S(1)}, bf16[512,256]{1,0:T(8,128)(2,1)S(1)}, u32[]{:S(2)}, u32[]{:S(2)}) %collective-permute-start.2) | collective-permute-done | bytes 262176 | tf_op jit(solution)/shard_map/ppermute | solution.py:36
  40.3 7.0 %all-to-all-done = bf16[8,256,256]{2,1,0:T(8,128)(2,1)S(1)} async-done(((bf16[8,256,256]{2,1,0:T(8,128)(2,1)}), bf16[8,256,256]{2,1,0:T(8,128)(2,1)S(1)}, u32[]{:S(2)}, u32[]{:S(2)}) %all-to-all-start) | async-done | bytes 1048608 | tf_op jit(solution)/shard_map/all_to_all | solution.py:27
  47.3 5.2 %stats.1 = f32[8,16,256]{2,1,0:T(8,128)S(1)} custom-call(s32[9]{0:T(128)S(1)} %pad_add_fusion.1.at_ref, bf16[2048,256]{1,0:T(8,128)(2,1)S(1)} %bitcast.32, bf16[2048,256]{1,0:T(8,128)(2,1)S(1)} %convolution_convert_fusion.users_ref, f32[8,8,256]{2,1,0:T(8,128)S(1)} %maximum_maximum_fusion.own_ref), custom_call_target="tpu_custom_call" | custom-call | tf_op jit(solution)/shard_map/stats/pallas_call | solution.py:79
  52.4 9.8 %all_to_all.25.got_ref = f32[8,16,256]{2,1,0:T(8,128)S(1)} all-to-all(f32[8,16,256]{2,1,0:T(8,128)S(1)} %stats.1), channel_id=1, replica_groups=mesh['z'=8,'x'=4,'k'=2,'y'=4] {'x','k'}, dimensions={0} | all-to-all | bytes 262144 | tf_op jit(solution)/shard_map/all_to_all | solution.py:27
  62.2 6.6 %user_side.1 = (bf16[2048,2048]{1,0:T(8,128)(2,1)S(1)}, f32[4,256,256]{2,1,0:T(8,128)S(1)}, f32[4,256,256]{2,1,0:T(8,128)}) custom-call(s32[9]{0:T(128)S(1)} %pad_add_fusion.1.at_ref, bf16[2048,256]{1,0:T(8,128)(2,1)S(1)} %bitcast.33, bf16[2048,256]{1,0:T(8,128)(2,1)S(1)} %convolution_convert_fusion.users_ref, f32[8,16,256]{2,1,0:T(8,128)S(1)} %all_to_all.25.got_ref), custom_call_target="tpu_custom_call" | custom-call | tf_op jit(solution)/shard_map/user_side/pallas_call | solution.py:117
  69.7 4.1 %item_side.1 = s16[8,264,256]{2,1,0:T(8,128)(2,1)} custom-call(bf16[2048,2048]{1,0:T(8,128)(2,1)S(1)} %get-tuple-element.12.all_ref, bf16[2048,256]{1,0:T(8,128)(2,1)S(1)} %convolution_convert_fusion.users_ref, f32[8,16,256]{2,1,0:T(8,128)S(1)} %all_to_all.25.got_ref), custom_call_target="tpu_custom_call" | custom-call | tf_op jit(solution)/shard_map/item_side/pallas_call | solution.py:153
  73.8 3.6 %all-to-all-start.3 = ((s16[8,264,256]{2,1,0:T(8,128)(2,1)}), s16[8,264,256]{2,1,0:T(8,128)(2,1)S(1)}, u32[]{:S(2)}, u32[]{:S(2)}) async-start(s16[8,264,256]{2,1,0:T(8,128)(2,1)} %item_side.1), calls=%async_computation.3 | async-start | bytes 2162688 | tf_op jit(solution)/shard_map/all_to_all | solution.py:27
  80.9 5.8 %collective-permute-done.8.one_ref = f32[256,256]{1,0:T(8,128)S(1)} collective-permute-done((f32[256,256]{1,0:T(8,128)S(1)}, f32[256,256]{1,0:T(8,128)S(1)}, u32[]{:S(2)}, u32[]{:S(2)}) %collective-permute-start.8) | collective-permute-done | bytes 262176 | tf_op jit(solution)/shard_map/ppermute | solution.py:36
  86.7 2.2 %collective-permute-done.9.two_ref = f32[256,256]{1,0:T(8,128)S(1)} collective-permute-done((f32[256,256]{1,0:T(8,128)S(1)}, f32[256,256]{1,0:T(8,128)S(1)}, u32[]{:S(2)}, u32[]{:S(2)}) %collective-permute-start.9) | collective-permute-done | bytes 262176 | tf_op jit(solution)/shard_map/ppermute | solution.py:36
  88.9 6.2 %collective-permute-done.10.three_ref = f32[256,256]{1,0:T(8,128)S(1)} collective-permute-done((f32[256,256]{1,0:T(8,128)S(1)}, f32[256,256]{1,0:T(8,128)S(1)}, u32[]{:S(2)}, u32[]{:S(2)}) %collective-permute-start.10) | collective-permute-done | bytes 262176 | tf_op jit(solution)/shard_map/ppermute | solution.py:36
  97.5 2.3 %collective-permute-start.14 = (f32[64,256]{1,0:T(8,128)S(1)}, f32[64,256]{1,0:T(8,128)S(1)}, u32[]{:S(2)}, u32[]{:S(2)}) collective-permute-start(f32[64,256]{1,0:T(8,128)S(1)} %get-tuple-element.19), channel_id=1, source_target_pairs={{0,3},{1,0},{2,1},{3,2},{4,7},{5,4},{6,5},{7,6},{8,11},{9,8},{10,9... | collective-permute-start | bytes 196616 | tf_op jit(solution)/shard_map/ppermute | solution.py:36
  101.4 3.3 %collective-permute-done.13 = f32[64,256]{1,0:T(8,128)S(1)} collective-permute-done((f32[64,256]{1,0:T(8,128)S(1)}, f32[64,256]{1,0:T(8,128)S(1)}, u32[]{:S(2)}, u32[]{:S(2)}) %collective-permute-start.13) | collective-permute-done | bytes 65568 | tf_op jit(solution)/shard_map/ppermute | solution.py:36
  114.6 2.3 %collective-permute-start.19 = (f32[16,256]{1,0:T(8,128)S(1)}, f32[16,256]{1,0:T(8,128)S(1)}, u32[]{:S(2)}, u32[]{:S(2)}) collective-permute-start(f32[16,256]{1,0:T(8,128)S(1)} %add.104), channel_id=1, source_target_pairs={{0,64},{32,96},{64,0},{96,32},{128,192},{160,224},{192,128},{224,1... | collective-permute-start | bytes 49160 | tf_op jit(solution)/shard_map/ppermute | solution.py:316
  118.1 5.5 %collective-permute-start.20 = (f32[16,256]{1,0:T(8,128)S(1)}, f32[16,256]{1,0:T(8,128)S(1)}, u32[]{:S(2)}, u32[]{:S(2)}) collective-permute-start(f32[16,256]{1,0:T(8,128)S(1)} %add.105), channel_id=1, source_target_pairs={{0,128},{32,160},{64,192},{96,224},{128,0},{160,32},{192,64},{224,... | collective-permute-start | bytes 49160 | tf_op jit(solution)/shard_map/ppermute | solution.py:316
  125.5 3.8 %all-to-all-start.2 = ((f32[16,16,256]{2,1,0:T(8,128)}), f32[16,16,256]{2,1,0:T(8,128)S(1)}, u32[]{:S(2)}, u32[]{:S(2)}) async-start(f32[16,16,256]{2,1,0:T(8,128)} %broadcast_in_dim.27), calls=%async_computation.2 | async-start | bytes 524288 | tf_op jit(solution)/shard_map/all_to_all | solution.py:27
  130.7 6.1 %all-to-all-done.2 = f32[16,16,256]{2,1,0:T(8,128)S(1)} async-done(((f32[16,16,256]{2,1,0:T(8,128)}), f32[16,16,256]{2,1,0:T(8,128)S(1)}, u32[]{:S(2)}, u32[]{:S(2)}) %all-to-all-start.2) | async-done | bytes 262176 | tf_op jit(solution)/shard_map/all_to_all | solution.py:27
  136.8 16.0 %all-to-all-start.4 = ((bf16[256,8,128]{2,1,0:T(8,128)(2,1)}), bf16[256,8,128]{2,1,0:T(8,128)(2,1)S(1)}, u32[]{:S(2)}, u32[]{:S(2)}) async-start(bf16[256,8,128]{2,1,0:T(8,128)(2,1)} %bitcast.15), calls=%async_computation.4 | async-start | bytes 1048576 | tf_op jit(solution)/shard_map/all_to_all | solution.py:27
  153.2 2.2 %collective-permute-start.21 = (f32[256,256]{1,0:T(8,128)S(1)}, f32[256,256]{1,0:T(8,128)S(1)}, u32[]{:S(2)}, u32[]{:S(2)}) collective-permute-start(f32[256,256]{1,0:T(8,128)S(1)} %bitcast.43), channel_id=1, source_target_pairs={{0,4},{4,0},{1,5},{5,1},{2,6},{6,2},{3,7},{7,3},{8,12},{12,8},{9,1... | collective-permute-start | bytes 786440 | tf_op jit(solution)/shard_map/ppermute | solution.py:36
  157.5 15.8 %all-to-all-done.4 = bf16[256,8,128]{2,1,0:T(8,128)(2,1)S(1)} async-done(((bf16[256,8,128]{2,1,0:T(8,128)(2,1)}), bf16[256,8,128]{2,1,0:T(8,128)(2,1)S(1)}, u32[]{:S(2)}, u32[]{:S(2)}) %all-to-all-start.4) | async-done | bytes 524320 | tf_op jit(solution)/shard_map/all_to_all | solution.py:27
  173.3 4.6 %table.1 = f32[64,4096]{1,0:T(8,128)} custom-call(bf16[2048,128]{1,0:T(8,128)(2,1)S(1)} %bitcast.34, s32[1,4096]{1,0:T(1,128)S(1)} %pad_add_fusion.ids_ref), custom_call_target="tpu_custom_call" | custom-call | tf_op jit(solution)/shard_map/table/pallas_call | solution.py:252
  (100 shorter events, 41.3 us)
Async XLA Ops:
  3.3 17.5 %collective-permute-start.4 = (f32[64,16]{1,0:T(8,128)S(1)}, f32[64,16]{1,0:T(8,128)S(1)}, u32[]{:S(2)}, u32[]{:S(2)}) collective-permute-start(f32[64,16]{1,0:T(8,128)S(1)} %convert_element_type.52), channel_id=1, source_target_pairs={{0,3},{1,0},{2,1},{3,2},{4,7},{5,4},{6,5},{7,6},{8,11},{9,8},{10,9... | collective-permute-start | bytes 12296 | tf_op jit(solution)/shard_map/ppermute | solution.py:36
  6.9 14.0 %collective-permute-start.5 = (f32[64,16]{1,0:T(8,128)S(1)}, f32[64,16]{1,0:T(8,128)S(1)}, u32[]{:S(2)}, u32[]{:S(2)}) collective-permute-start(f32[64,16]{1,0:T(8,128)S(1)} %convert_element_type.52), channel_id=1, source_target_pairs={{0,2},{1,3},{2,0},{3,1},{4,6},{5,7},{6,4},{7,5},{8,10},{9,11},{10,... | collective-permute-start | bytes 12296 | tf_op jit(solution)/shard_map/ppermute | solution.py:36
  7.3 13.6 %collective-permute-start.6 = (f32[64,16]{1,0:T(8,128)S(1)}, f32[64,16]{1,0:T(8,128)S(1)}, u32[]{:S(2)}, u32[]{:S(2)}) collective-permute-start(f32[64,16]{1,0:T(8,128)S(1)} %convert_element_type.52), channel_id=1, source_target_pairs={{0,1},{1,2},{2,3},{3,0},{4,5},{5,6},{6,7},{7,4},{8,9},{9,10},{10,1... | collective-permute-start | bytes 12296 | tf_op jit(solution)/shard_map/ppermute | solution.py:36
  9.9 37.4 %all-to-all-start = ((bf16[8,256,256]{2,1,0:T(8,128)(2,1)}), bf16[8,256,256]{2,1,0:T(8,128)(2,1)S(1)}, u32[]{:S(2)}, u32[]{:S(2)}) async-start(bf16[8,256,256]{2,1,0:T(8,128)(2,1)} %broadcast_in_dim.11), calls=%async_computation | async-start | bytes 2097152 | tf_op jit(solution)/shard_map/all_to_all | solution.py:27
  18.1 3.0 %collective-permute-start = (bf16[256,256]{1,0:T(8,128)(2,1)S(1)}, bf16[256,256]{1,0:T(8,128)(2,1)S(1)}, u32[]{:S(2)}, u32[]{:S(2)}) collective-permute-start(bf16[256,256]{1,0:T(8,128)(2,1)S(1)} %bitcast.35), channel_id=1, source_target_pairs={{0,4},{4,0},{1,5},{5,1},{2,6},{6,2},{3,7},{7,3},{8,12},{12,8},{9,1... | collective-permute-start | bytes 393224 | tf_op jit(solution)/shard_map/ppermute | solution.py:36
  21.2 9.0 %collective-permute-start.1 = (bf16[512,256]{1,0:T(8,128)(2,1)S(1)}, bf16[512,256]{1,0:T(8,128)(2,1)S(1)}, u32[]{:S(2)}, u32[]{:S(2)}) collective-permute-start(bf16[512,256]{1,0:T(8,128)(2,1)S(1)} %pad_maximum_fusion), channel_id=1, source_target_pairs={{0,8},{8,16},{16,24},{24,0},{1,9},{9,17},{17,25},{25,1},{2,10},{10... | collective-permute-start | bytes 786440 | tf_op jit(solution)/shard_map/ppermute | solution.py:36
  22.5 14.3 %collective-permute-start.2 = (bf16[512,256]{1,0:T(8,128)(2,1)S(1)}, bf16[512,256]{1,0:T(8,128)(2,1)S(1)}, u32[]{:S(2)}, u32[]{:S(2)}) collective-permute-start(bf16[512,256]{1,0:T(8,128)(2,1)S(1)} %pad_maximum_fusion), channel_id=1, source_target_pairs={{0,16},{8,24},{16,0},{24,8},{1,17},{9,25},{17,1},{25,9},{2,18},{10... | collective-permute-start | bytes 786440 | tf_op jit(solution)/shard_map/ppermute | solution.py:36
  25.0 12.5 %collective-permute-start.3 = (bf16[512,256]{1,0:T(8,128)(2,1)S(1)}, bf16[512,256]{1,0:T(8,128)(2,1)S(1)}, u32[]{:S(2)}, u32[]{:S(2)}) collective-permute-start(bf16[512,256]{1,0:T(8,128)(2,1)S(1)} %pad_maximum_fusion), channel_id=1, source_target_pairs={{0,24},{8,0},{16,8},{24,16},{1,25},{9,1},{17,9},{25,17},{2,26},{10... | collective-permute-start | bytes 786440 | tf_op jit(solution)/shard_map/ppermute | solution.py:36
  68.9 8.5 %collective-permute-start.7 = (f32[4,256,256]{2,1,0:T(8,128)}, f32[4,256,256]{2,1,0:T(8,128)}, u32[]{:S(2)}, u32[]{:S(2)}) collective-permute-start(f32[4,256,256]{2,1,0:T(8,128)} %get-tuple-element.9), channel_id=1, source_target_pairs={{0,4},{4,0},{1,5},{5,1},{2,6},{6,2},{3,7},{7,3},{8,12},{12,8},{9,1... | collective-permute-start | bytes 3145736 | tf_op jit(solution)/shard_map/ppermute | solution.py:36
  73.8 51.0 %all-to-all-start.3 = ((s16[8,264,256]{2,1,0:T(8,128)(2,1)}), s16[8,264,256]{2,1,0:T(8,128)(2,1)S(1)}, u32[]{:S(2)}, u32[]{:S(2)}) async-start(s16[8,264,256]{2,1,0:T(8,128)(2,1)} %item_side.1), calls=%async_computation.3 | async-start | bytes 2162688 | tf_op jit(solution)/shard_map/all_to_all | solution.py:27
  78.8 7.9 %collective-permute-start.8 = (f32[256,256]{1,0:T(8,128)S(1)}, f32[256,256]{1,0:T(8,128)S(1)}, u32[]{:S(2)}, u32[]{:S(2)}) collective-permute-start(f32[256,256]{1,0:T(8,128)S(1)} %get-tuple-element.15), channel_id=1, source_target_pairs={{0,24},{8,0},{16,8},{24,16},{1,25},{9,1},{17,9},{25,17},{2,26},{10... | collective-permute-start | bytes 786440 | tf_op jit(solution)/shard_map/ppermute | solution.py:36
  79.7 9.1 %collective-permute-start.9 = (f32[256,256]{1,0:T(8,128)S(1)}, f32[256,256]{1,0:T(8,128)S(1)}, u32[]{:S(2)}, u32[]{:S(2)}) collective-permute-start(f32[256,256]{1,0:T(8,128)S(1)} %get-tuple-element.14), channel_id=1, source_target_pairs={{0,16},{8,24},{16,0},{24,8},{1,17},{9,25},{17,1},{25,9},{2,18},{10... | collective-permute-start | bytes 786440 | tf_op jit(solution)/shard_map/ppermute | solution.py:36
  80.9 14.2 %collective-permute-start.10 = (f32[256,256]{1,0:T(8,128)S(1)}, f32[256,256]{1,0:T(8,128)S(1)}, u32[]{:S(2)}, u32[]{:S(2)}) collective-permute-start(f32[256,256]{1,0:T(8,128)S(1)} %get-tuple-element.13), channel_id=1, source_target_pairs={{0,8},{8,16},{16,24},{24,0},{1,9},{9,17},{17,25},{25,1},{2,10},{10... | collective-permute-start | bytes 786440 | tf_op jit(solution)/shard_map/ppermute | solution.py:36
  97.5 3.9 %collective-permute-start.14 = (f32[64,256]{1,0:T(8,128)S(1)}, f32[64,256]{1,0:T(8,128)S(1)}, u32[]{:S(2)}, u32[]{:S(2)}) collective-permute-start(f32[64,256]{1,0:T(8,128)S(1)} %get-tuple-element.19), channel_id=1, source_target_pairs={{0,3},{1,0},{2,1},{3,2},{4,7},{5,4},{6,5},{7,6},{8,11},{9,8},{10,9... | collective-permute-start | bytes 196616 | tf_op jit(solution)/shard_map/ppermute | solution.py:36
  99.8 4.9 %collective-permute-start.13 = (f32[64,256]{1,0:T(8,128)S(1)}, f32[64,256]{1,0:T(8,128)S(1)}, u32[]{:S(2)}, u32[]{:S(2)}) collective-permute-start(f32[64,256]{1,0:T(8,128)S(1)} %get-tuple-element.20), channel_id=1, source_target_pairs={{0,2},{1,3},{2,0},{3,1},{4,6},{5,7},{6,4},{7,5},{8,10},{9,11},{10,... | collective-permute-start | bytes 196616 | tf_op jit(solution)/shard_map/ppermute | solution.py:36
  101.2 5.3 %collective-permute-start.12 = (f32[64,256]{1,0:T(8,128)S(1)}, f32[64,256]{1,0:T(8,128)S(1)}, u32[]{:S(2)}, u32[]{:S(2)}) collective-permute-start(f32[64,256]{1,0:T(8,128)S(1)} %get-tuple-element.18), channel_id=1, source_target_pairs={{0,1},{1,2},{2,3},{3,0},{4,5},{5,6},{6,7},{7,4},{8,9},{9,10},{10,1... | collective-permute-start | bytes 196616 | tf_op jit(solution)/shard_map/ppermute | solution.py:36
  106.9 4.1 %collective-permute-start.16 = (f32[16,256]{1,0:T(8,128)S(1)}, f32[16,256]{1,0:T(8,128)S(1)}, u32[]{:S(2)}, u32[]{:S(2)}) collective-permute-start(f32[16,256]{1,0:T(8,128)S(1)} %get-tuple-element.25), channel_id=1, source_target_pairs={{0,16},{8,24},{16,0},{24,8},{1,17},{9,25},{17,1},{25,9},{2,18},{10... | collective-permute-start | bytes 49160 | tf_op jit(solution)/shard_map/ppermute | solution.py:36
  108.1 3.8 %collective-permute-start.15 = (f32[16,256]{1,0:T(8,128)S(1)}, f32[16,256]{1,0:T(8,128)S(1)}, u32[]{:S(2)}, u32[]{:S(2)}) collective-permute-start(f32[16,256]{1,0:T(8,128)S(1)} %get-tuple-element.23), channel_id=1, source_target_pairs={{0,8},{8,16},{16,24},{24,0},{1,9},{9,17},{17,25},{25,1},{2,10},{10... | collective-permute-start | bytes 49160 | tf_op jit(solution)/shard_map/ppermute | solution.py:36
  111.9 2.7 %collective-permute-start.18 = (f32[16,256]{1,0:T(8,128)S(1)}, f32[16,256]{1,0:T(8,128)S(1)}, u32[]{:S(2)}, u32[]{:S(2)}) collective-permute-start(f32[16,256]{1,0:T(8,128)S(1)} %add_add_fusion.1), channel_id=1, source_target_pairs={{0,32},{32,0},{64,96},{96,64},{128,160},{160,128},{192,224},{224,1... | collective-permute-start | bytes 49160 | tf_op jit(solution)/shard_map/ppermute | solution.py:316
  114.6 3.5 %collective-permute-start.19 = (f32[16,256]{1,0:T(8,128)S(1)}, f32[16,256]{1,0:T(8,128)S(1)}, u32[]{:S(2)}, u32[]{:S(2)}) collective-permute-start(f32[16,256]{1,0:T(8,128)S(1)} %add.104), channel_id=1, source_target_pairs={{0,64},{32,96},{64,0},{96,32},{128,192},{160,224},{192,128},{224,1... | collective-permute-start | bytes 49160 | tf_op jit(solution)/shard_map/ppermute | solution.py:316
  118.1 6.6 %collective-permute-start.20 = (f32[16,256]{1,0:T(8,128)S(1)}, f32[16,256]{1,0:T(8,128)S(1)}, u32[]{:S(2)}, u32[]{:S(2)}) collective-permute-start(f32[16,256]{1,0:T(8,128)S(1)} %add.105), channel_id=1, source_target_pairs={{0,128},{32,160},{64,192},{96,224},{128,0},{160,32},{192,64},{224,... | collective-permute-start | bytes 49160 | tf_op jit(solution)/shard_map/ppermute | solution.py:316
  125.5 11.3 %all-to-all-start.2 = ((f32[16,16,256]{2,1,0:T(8,128)}), f32[16,16,256]{2,1,0:T(8,128)S(1)}, u32[]{:S(2)}, u32[]{:S(2)}) async-start(f32[16,16,256]{2,1,0:T(8,128)} %broadcast_in_dim.27), calls=%async_computation.2 | async-start | bytes 524288 | tf_op jit(solution)/shard_map/all_to_all | solution.py:27
  136.8 36.5 %all-to-all-start.4 = ((bf16[256,8,128]{2,1,0:T(8,128)(2,1)}), bf16[256,8,128]{2,1,0:T(8,128)(2,1)S(1)}, u32[]{:S(2)}, u32[]{:S(2)}) async-start(bf16[256,8,128]{2,1,0:T(8,128)(2,1)} %bitcast.15), calls=%async_computation.4 | async-start | bytes 1048576 | tf_op jit(solution)/shard_map/all_to_all | solution.py:27
  153.2 3.4 %collective-permute-start.21 = (f32[256,256]{1,0:T(8,128)S(1)}, f32[256,256]{1,0:T(8,128)S(1)}, u32[]{:S(2)}, u32[]{:S(2)}) collective-permute-start(f32[256,256]{1,0:T(8,128)S(1)} %bitcast.43), channel_id=1, source_target_pairs={{0,4},{4,0},{1,5},{5,1},{2,6},{6,2},{3,7},{7,3},{8,12},{12,8},{9,1... | collective-permute-start | bytes 786440 | tf_op jit(solution)/shard_map/ppermute | solution.py:36
  (8 other events, 136.3 us)

commit v4 on v3

--- a/solution.py
+++ b/solution.py
@@ -126,10 +126,11 @@
 
 
 def items_kernel(all_ref, users_ref, got_ref, gi_ref, ids_ref):
-    gi = dot(all_ref[...], users_ref[...], (1, 0))
     ids_ref[...] = jnp.zeros_like(ids_ref)
     for z in range(8):
-        part = gi[z * BLK : (z + 1) * BLK]
+        if z % 2 == 0:
+            pair = dot(all_ref[z * BLK : (z + 2) * BLK, :], users_ref[...], (1, 0))
+        part = pair[:BLK] if z % 2 == 0 else pair[BLK:]
         largest = jnp.maximum(jnp.max(jnp.abs(part), axis=0, keepdims=True), 1e-30)
         power = jnp.ceil(jnp.log(largest) * 1.4426950408889634)
         whole = jnp.floor(part * jnp.exp2(14.9 - power) + 0.5)
@@ -312,7 +313,7 @@
     both = both + shifted(other, "k", 1)
     both = summed_share(both, "y")
     both = summed_share(both, "x")
-    for step in (1, 2, 4):
+    for step in (1, 2, 7):
         both = both + lax.ppermute(both, "z", [(i, i ^ step) for i in range(8)])
 
     send = pack(gi, owner, rank).reshape(256, 8, 128)

time: 178 us -> 176 us (0.989)
  starting transfers between devices: 63.7 us -> 61.5 us
    ppermute x3, starting transfers between devices: 9.15 us -> 6.3 us  [step_body(): both = both + lax.ppermute(both, 'z', [(i, i ^ step) for i in range(8)])]
where the time goes in v4:
time: 176 us; the launch traced here: 175 us
  waiting for transfers between devices  66.9 us (38%)
  starting transfers between devices  61.5 us (35%)
  Pallas kernels  22.2 us (13%)
  blocking collectives  9.82 us (6%)
  local copies, waits for them, and re-layouts  7.01 us (4%)
  other arithmetic  4.12 us (2%)
  matrix products  2.98 us (2%)
    ppermute x19, waiting for transfers between devices, shifted(): lax.ppermute(value, axis, [(i, (i + step) % count) for i in range(count)])  34.3 us
    all_to_all x4, starting transfers between devices, exchange(): return lax.all_to_all(value, axes, 0, 0, tiled=True)  32.3 us
    all_to_all x4, waiting for transfers between devices, exchange(): return lax.all_to_all(value, axes, 0, 0, tiled=True)  28.9 us
    ppermute x19, starting transfers between devices, shifted(): lax.ppermute(value, axis, [(i, (i + step) % count) for i in range(count)])  22.9 us
    all_to_all x1, blocking collectives, exchange(): return lax.all_to_all(value, axes, 0, 0, tiled=True)  9.82 us
    pallas_call x1, Pallas kernels, user_side(): pl.pallas_call(users_kernel, in_specs=[SMEM, VMEM, VMEM, VMEM], out_specs...  6.61 us
    ppermute x3, starting transfers between devices, step_body(): both = both + lax.ppermute(both, 'z', [(i, i ^ step) for i in range(8)])  6.3 us
    pallas_call x1, Pallas kernels, stats(): pl.pallas_call(stats_kernel, in_specs=[SMEM, VMEM, VMEM, VMEM], out_specs...  5.16 us
  transfers between devices with their start and end apart: 26, of which 19 were waited for; matrix products, arithmetic and copies ran while one was open for 6% of the time, Pallas kernels for 3%

profile of v4, /device:TPU:1, one launch (start us, length us, event | category | flops | bytes accessed | tf_op | source)
XLA Modules:
  0.0 175.4 jit_solution(4430523896389449147)
XLA Ops:
  3.3 3.6 %collective-permute-start.4 = (f32[64,16]{1,0:T(8,128)S(1)}, f32[64,16]{1,0:T(8,128)S(1)}, u32[]{:S(2)}, u32[]{:S(2)}) collective-permute-start(f32[64,16]{1,0:T(8,128)S(1)} %convert_element_type.52), channel_id=1, source_target_pairs={{0,3},{1,0},{2,1},{3,2},{4,7},{5,4},{6,5},{7,6},{8,11},{9,8},{10,9... | collective-permute-start | bytes 12296 | tf_op jit(solution)/shard_map/ppermute | solution.py:36
  9.9 8.2 %all-to-all-start = ((bf16[8,256,256]{2,1,0:T(8,128)(2,1)}), bf16[8,256,256]{2,1,0:T(8,128)(2,1)S(1)}, u32[]{:S(2)}, u32[]{:S(2)}) async-start(bf16[8,256,256]{2,1,0:T(8,128)(2,1)} %broadcast_in_dim.11), calls=%async_computation | async-start | bytes 2097152 | tf_op jit(solution)/shard_map/all_to_all | solution.py:27
  22.5 2.5 %collective-permute-start.2 = (bf16[512,256]{1,0:T(8,128)(2,1)S(1)}, bf16[512,256]{1,0:T(8,128)(2,1)S(1)}, u32[]{:S(2)}, u32[]{:S(2)}) collective-permute-start(bf16[512,256]{1,0:T(8,128)(2,1)S(1)} %pad_maximum_fusion), channel_id=1, source_target_pairs={{0,16},{8,24},{16,0},{24,8},{1,17},{9,25},{17,1},{25,9},{2,18},{10... | collective-permute-start | bytes 786440 | tf_op jit(solution)/shard_map/ppermute | solution.py:36
  26.8 3.3 %collective-permute-done.1 = bf16[512,256]{1,0:T(8,128)(2,1)S(1)} collective-permute-done((bf16[512,256]{1,0:T(8,128)(2,1)S(1)}, bf16[512,256]{1,0:T(8,128)(2,1)S(1)}, u32[]{:S(2)}, u32[]{:S(2)}) %collective-permute-start.1) | collective-permute-done | bytes 262176 | tf_op jit(solution)/shard_map/ppermute | solution.py:36
  30.9 5.9 %collective-permute-done.2 = bf16[512,256]{1,0:T(8,128)(2,1)S(1)} collective-permute-done((bf16[512,256]{1,0:T(8,128)(2,1)S(1)}, bf16[512,256]{1,0:T(8,128)(2,1)S(1)}, u32[]{:S(2)}, u32[]{:S(2)}) %collective-permute-start.2) | collective-permute-done | bytes 262176 | tf_op jit(solution)/shard_map/ppermute | solution.py:36
  40.3 7.0 %all-to-all-done = bf16[8,256,256]{2,1,0:T(8,128)(2,1)S(1)} async-done(((bf16[8,256,256]{2,1,0:T(8,128)(2,1)}), bf16[8,256,256]{2,1,0:T(8,128)(2,1)S(1)}, u32[]{:S(2)}, u32[]{:S(2)}) %all-to-all-start) | async-done | bytes 1048608 | tf_op jit(solution)/shard_map/all_to_all | solution.py:27
  47.3 5.2 %stats.1 = f32[8,16,256]{2,1,0:T(8,128)S(1)} custom-call(s32[9]{0:T(128)S(1)} %pad_add_fusion.1.at_ref, bf16[2048,256]{1,0:T(8,128)(2,1)S(1)} %bitcast.32, bf16[2048,256]{1,0:T(8,128)(2,1)S(1)} %convolution_convert_fusion.users_ref, f32[8,8,256]{2,1,0:T(8,128)S(1)} %maximum_maximum_fusion.own_ref), custom_call_target="tpu_custom_call" | custom-call | tf_op jit(solution)/shard_map/stats/pallas_call | solution.py:79
  52.4 9.8 %all_to_all.25.got_ref = f32[8,16,256]{2,1,0:T(8,128)S(1)} all-to-all(f32[8,16,256]{2,1,0:T(8,128)S(1)} %stats.1), channel_id=1, replica_groups=mesh['z'=8,'x'=4,'k'=2,'y'=4] {'x','k'}, dimensions={0} | all-to-all | bytes 262144 | tf_op jit(solution)/shard_map/all_to_all | solution.py:27
  62.2 6.6 %user_side.1 = (bf16[2048,2048]{1,0:T(8,128)(2,1)S(1)}, f32[4,256,256]{2,1,0:T(8,128)S(1)}, f32[4,256,256]{2,1,0:T(8,128)}) custom-call(s32[9]{0:T(128)S(1)} %pad_add_fusion.1.at_ref, bf16[2048,256]{1,0:T(8,128)(2,1)S(1)} %bitcast.33, bf16[2048,256]{1,0:T(8,128)(2,1)S(1)} %convolution_convert_fusion.users_ref, f32[8,16,256]{2,1,0:T(8,128)S(1)} %all_to_all.25.got_ref), custom_call_target="tpu_custom_call" | custom-call | tf_op jit(solution)/shard_map/user_side/pallas_call | solution.py:117
  69.7 3.9 %item_side.1 = s16[8,264,256]{2,1,0:T(8,128)(2,1)} custom-call(bf16[2048,2048]{1,0:T(8,128)(2,1)S(1)} %get-tuple-element.12.all_ref, bf16[2048,256]{1,0:T(8,128)(2,1)S(1)} %convolution_convert_fusion.users_ref, f32[8,16,256]{2,1,0:T(8,128)S(1)} %all_to_all.25.got_ref), custom_call_target="tpu_custom_call" | custom-call | tf_op jit(solution)/shard_map/item_side/pallas_call | solution.py:154
  73.6 3.6 %all-to-all-start.3 = ((s16[8,264,256]{2,1,0:T(8,128)(2,1)}), s16[8,264,256]{2,1,0:T(8,128)(2,1)S(1)}, u32[]{:S(2)}, u32[]{:S(2)}) async-start(s16[8,264,256]{2,1,0:T(8,128)(2,1)} %item_side.1), calls=%async_computation.3 | async-start | bytes 2162688 | tf_op jit(solution)/shard_map/all_to_all | solution.py:27
  80.8 5.8 %collective-permute-done.8.one_ref = f32[256,256]{1,0:T(8,128)S(1)} collective-permute-done((f32[256,256]{1,0:T(8,128)S(1)}, f32[256,256]{1,0:T(8,128)S(1)}, u32[]{:S(2)}, u32[]{:S(2)}) %collective-permute-start.8) | collective-permute-done | bytes 262176 | tf_op jit(solution)/shard_map/ppermute | solution.py:36
  86.5 2.2 %collective-permute-done.9.two_ref = f32[256,256]{1,0:T(8,128)S(1)} collective-permute-done((f32[256,256]{1,0:T(8,128)S(1)}, f32[256,256]{1,0:T(8,128)S(1)}, u32[]{:S(2)}, u32[]{:S(2)}) %collective-permute-start.9) | collective-permute-done | bytes 262176 | tf_op jit(solution)/shard_map/ppermute | solution.py:36
  88.7 6.2 %collective-permute-done.10.three_ref = f32[256,256]{1,0:T(8,128)S(1)} collective-permute-done((f32[256,256]{1,0:T(8,128)S(1)}, f32[256,256]{1,0:T(8,128)S(1)}, u32[]{:S(2)}, u32[]{:S(2)}) %collective-permute-start.10) | collective-permute-done | bytes 262176 | tf_op jit(solution)/shard_map/ppermute | solution.py:36
  97.3 2.1 %collective-permute-start.14 = (f32[64,256]{1,0:T(8,128)S(1)}, f32[64,256]{1,0:T(8,128)S(1)}, u32[]{:S(2)}, u32[]{:S(2)}) collective-permute-start(f32[64,256]{1,0:T(8,128)S(1)} %get-tuple-element.19), channel_id=1, source_target_pairs={{0,3},{1,0},{2,1},{3,2},{4,7},{5,4},{6,5},{7,6},{8,11},{9,8},{10,9... | collective-permute-start | bytes 196616 | tf_op jit(solution)/shard_map/ppermute | solution.py:36
  101.0 3.3 %collective-permute-done.13 = f32[64,256]{1,0:T(8,128)S(1)} collective-permute-done((f32[64,256]{1,0:T(8,128)S(1)}, f32[64,256]{1,0:T(8,128)S(1)}, u32[]{:S(2)}, u32[]{:S(2)}) %collective-permute-start.13) | collective-permute-done | bytes 65568 | tf_op jit(solution)/shard_map/ppermute | solution.py:36
  114.2 2.3 %collective-permute-start.19 = (f32[16,256]{1,0:T(8,128)S(1)}, f32[16,256]{1,0:T(8,128)S(1)}, u32[]{:S(2)}, u32[]{:S(2)}) collective-permute-start(f32[16,256]{1,0:T(8,128)S(1)} %add.104), channel_id=1, source_target_pairs={{0,64},{32,96},{64,0},{96,32},{128,192},{160,224},{192,128},{224,1... | collective-permute-start | bytes 49160 | tf_op jit(solution)/shard_map/ppermute | solution.py:317
  117.7 2.6 %collective-permute-start.20 = (f32[16,256]{1,0:T(8,128)S(1)}, f32[16,256]{1,0:T(8,128)S(1)}, u32[]{:S(2)}, u32[]{:S(2)}) collective-permute-start(f32[16,256]{1,0:T(8,128)S(1)} %add.105), channel_id=1, source_target_pairs={{0,224},{32,192},{64,160},{96,128},{128,96},{160,64},{192,32},{224... | collective-permute-start | bytes 49160 | tf_op jit(solution)/shard_map/ppermute | solution.py:317
  122.3 3.8 %all-to-all-start.2 = ((f32[16,16,256]{2,1,0:T(8,128)}), f32[16,16,256]{2,1,0:T(8,128)S(1)}, u32[]{:S(2)}, u32[]{:S(2)}) async-start(f32[16,16,256]{2,1,0:T(8,128)} %broadcast_in_dim.27), calls=%async_computation.2 | async-start | bytes 524288 | tf_op jit(solution)/shard_map/all_to_all | solution.py:27
  127.5 6.1 %all-to-all-done.2 = f32[16,16,256]{2,1,0:T(8,128)S(1)} async-done(((f32[16,16,256]{2,1,0:T(8,128)}), f32[16,16,256]{2,1,0:T(8,128)S(1)}, u32[]{:S(2)}, u32[]{:S(2)}) %all-to-all-start.2) | async-done | bytes 262176 | tf_op jit(solution)/shard_map/all_to_all | solution.py:27
  133.6 16.8 %all-to-all-start.4 = ((bf16[256,8,128]{2,1,0:T(8,128)(2,1)}), bf16[256,8,128]{2,1,0:T(8,128)(2,1)S(1)}, u32[]{:S(2)}, u32[]{:S(2)}) async-start(bf16[256,8,128]{2,1,0:T(8,128)(2,1)} %bitcast.15), calls=%async_computation.4 | async-start | bytes 1048576 | tf_op jit(solution)/shard_map/all_to_all | solution.py:27
  150.9 2.2 %collective-permute-start.21 = (f32[256,256]{1,0:T(8,128)S(1)}, f32[256,256]{1,0:T(8,128)S(1)}, u32[]{:S(2)}, u32[]{:S(2)}) collective-permute-start(f32[256,256]{1,0:T(8,128)S(1)} %bitcast.43), channel_id=1, source_target_pairs={{0,4},{4,0},{1,5},{5,1},{2,6},{6,2},{3,7},{7,3},{8,12},{12,8},{9,1... | collective-permute-start | bytes 786440 | tf_op jit(solution)/shard_map/ppermute | solution.py:36
  155.1 15.8 %all-to-all-done.4 = bf16[256,8,128]{2,1,0:T(8,128)(2,1)S(1)} async-done(((bf16[256,8,128]{2,1,0:T(8,128)(2,1)}), bf16[256,8,128]{2,1,0:T(8,128)(2,1)S(1)}, u32[]{:S(2)}, u32[]{:S(2)}) %all-to-all-start.4) | async-done | bytes 524320 | tf_op jit(solution)/shard_map/all_to_all | solution.py:27
  170.9 4.6 %table.1 = f32[64,4096]{1,0:T(8,128)} custom-call(bf16[2048,128]{1,0:T(8,128)(2,1)S(1)} %bitcast.34, s32[1,4096]{1,0:T(1,128)S(1)} %pad_add_fusion.ids_ref), custom_call_target="tpu_custom_call" | custom-call | tf_op jit(solution)/shard_map/table/pallas_call | solution.py:253
  (100 shorter events, 41.3 us)
Async XLA Ops:
  3.3 17.5 %collective-permute-start.4 = (f32[64,16]{1,0:T(8,128)S(1)}, f32[64,16]{1,0:T(8,128)S(1)}, u32[]{:S(2)}, u32[]{:S(2)}) collective-permute-start(f32[64,16]{1,0:T(8,128)S(1)} %convert_element_type.52), channel_id=1, source_target_pairs={{0,3},{1,0},{2,1},{3,2},{4,7},{5,4},{6,5},{7,6},{8,11},{9,8},{10,9... | collective-permute-start | bytes 12296 | tf_op jit(solution)/shard_map/ppermute | solution.py:36
  6.9 14.0 %collective-permute-start.5 = (f32[64,16]{1,0:T(8,128)S(1)}, f32[64,16]{1,0:T(8,128)S(1)}, u32[]{:S(2)}, u32[]{:S(2)}) collective-permute-start(f32[64,16]{1,0:T(8,128)S(1)} %convert_element_type.52), channel_id=1, source_target_pairs={{0,2},{1,3},{2,0},{3,1},{4,6},{5,7},{6,4},{7,5},{8,10},{9,11},{10,... | collective-permute-start | bytes 12296 | tf_op jit(solution)/shard_map/ppermute | solution.py:36
  7.3 13.6 %collective-permute-start.6 = (f32[64,16]{1,0:T(8,128)S(1)}, f32[64,16]{1,0:T(8,128)S(1)}, u32[]{:S(2)}, u32[]{:S(2)}) collective-permute-start(f32[64,16]{1,0:T(8,128)S(1)} %convert_element_type.52), channel_id=1, source_target_pairs={{0,1},{1,2},{2,3},{3,0},{4,5},{5,6},{6,7},{7,4},{8,9},{9,10},{10,1... | collective-permute-start | bytes 12296 | tf_op jit(solution)/shard_map/ppermute | solution.py:36
  9.9 37.4 %all-to-all-start = ((bf16[8,256,256]{2,1,0:T(8,128)(2,1)}), bf16[8,256,256]{2,1,0:T(8,128)(2,1)S(1)}, u32[]{:S(2)}, u32[]{:S(2)}) async-start(bf16[8,256,256]{2,1,0:T(8,128)(2,1)} %broadcast_in_dim.11), calls=%async_computation | async-start | bytes 2097152 | tf_op jit(solution)/shard_map/all_to_all | solution.py:27
  18.1 3.0 %collective-permute-start = (bf16[256,256]{1,0:T(8,128)(2,1)S(1)}, bf16[256,256]{1,0:T(8,128)(2,1)S(1)}, u32[]{:S(2)}, u32[]{:S(2)}) collective-permute-start(bf16[256,256]{1,0:T(8,128)(2,1)S(1)} %bitcast.35), channel_id=1, source_target_pairs={{0,4},{4,0},{1,5},{5,1},{2,6},{6,2},{3,7},{7,3},{8,12},{12,8},{9,1... | collective-permute-start | bytes 393224 | tf_op jit(solution)/shard_map/ppermute | solution.py:36
  21.2 9.0 %collective-permute-start.1 = (bf16[512,256]{1,0:T(8,128)(2,1)S(1)}, bf16[512,256]{1,0:T(8,128)(2,1)S(1)}, u32[]{:S(2)}, u32[]{:S(2)}) collective-permute-start(bf16[512,256]{1,0:T(8,128)(2,1)S(1)} %pad_maximum_fusion), channel_id=1, source_target_pairs={{0,8},{8,16},{16,24},{24,0},{1,9},{9,17},{17,25},{25,1},{2,10},{10... | collective-permute-start | bytes 786440 | tf_op jit(solution)/shard_map/ppermute | solution.py:36
  22.5 14.3 %collective-permute-start.2 = (bf16[512,256]{1,0:T(8,128)(2,1)S(1)}, bf16[512,256]{1,0:T(8,128)(2,1)S(1)}, u32[]{:S(2)}, u32[]{:S(2)}) collective-permute-start(bf16[512,256]{1,0:T(8,128)(2,1)S(1)} %pad_maximum_fusion), channel_id=1, source_target_pairs={{0,16},{8,24},{16,0},{24,8},{1,17},{9,25},{17,1},{25,9},{2,18},{10... | collective-permute-start | bytes 786440 | tf_op jit(solution)/shard_map/ppermute | solution.py:36
  25.0 12.5 %collective-permute-start.3 = (bf16[512,256]{1,0:T(8,128)(2,1)S(1)}, bf16[512,256]{1,0:T(8,128)(2,1)S(1)}, u32[]{:S(2)}, u32[]{:S(2)}) collective-permute-start(bf16[512,256]{1,0:T(8,128)(2,1)S(1)} %pad_maximum_fusion), channel_id=1, source_target_pairs={{0,24},{8,0},{16,8},{24,16},{1,25},{9,1},{17,9},{25,17},{2,26},{10... | collective-permute-start | bytes 786440 | tf_op jit(solution)/shard_map/ppermute | solution.py:36
  68.9 8.3 %collective-permute-start.7 = (f32[4,256,256]{2,1,0:T(8,128)}, f32[4,256,256]{2,1,0:T(8,128)}, u32[]{:S(2)}, u32[]{:S(2)}) collective-permute-start(f32[4,256,256]{2,1,0:T(8,128)} %get-tuple-element.9), channel_id=1, source_target_pairs={{0,4},{4,0},{1,5},{5,1},{2,6},{6,2},{3,7},{7,3},{8,12},{12,8},{9,1... | collective-permute-start | bytes 3145736 | tf_op jit(solution)/shard_map/ppermute | solution.py:36
  73.6 47.9 %all-to-all-start.3 = ((s16[8,264,256]{2,1,0:T(8,128)(2,1)}), s16[8,264,256]{2,1,0:T(8,128)(2,1)S(1)}, u32[]{:S(2)}, u32[]{:S(2)}) async-start(s16[8,264,256]{2,1,0:T(8,128)(2,1)} %item_side.1), calls=%async_computation.3 | async-start | bytes 2162688 | tf_op jit(solution)/shard_map/all_to_all | solution.py:27
  78.6 7.9 %collective-permute-start.8 = (f32[256,256]{1,0:T(8,128)S(1)}, f32[256,256]{1,0:T(8,128)S(1)}, u32[]{:S(2)}, u32[]{:S(2)}) collective-permute-start(f32[256,256]{1,0:T(8,128)S(1)} %get-tuple-element.15), channel_id=1, source_target_pairs={{0,24},{8,0},{16,8},{24,16},{1,25},{9,1},{17,9},{25,17},{2,26},{10... | collective-permute-start | bytes 786440 | tf_op jit(solution)/shard_map/ppermute | solution.py:36
  79.6 9.1 %collective-permute-start.9 = (f32[256,256]{1,0:T(8,128)S(1)}, f32[256,256]{1,0:T(8,128)S(1)}, u32[]{:S(2)}, u32[]{:S(2)}) collective-permute-start(f32[256,256]{1,0:T(8,128)S(1)} %get-tuple-element.14), channel_id=1, source_target_pairs={{0,16},{8,24},{16,0},{24,8},{1,17},{9,25},{17,1},{25,9},{2,18},{10... | collective-permute-start | bytes 786440 | tf_op jit(solution)/shard_map/ppermute | solution.py:36
  80.7 14.2 %collective-permute-start.10 = (f32[256,256]{1,0:T(8,128)S(1)}, f32[256,256]{1,0:T(8,128)S(1)}, u32[]{:S(2)}, u32[]{:S(2)}) collective-permute-start(f32[256,256]{1,0:T(8,128)S(1)} %get-tuple-element.13), channel_id=1, source_target_pairs={{0,8},{8,16},{16,24},{24,0},{1,9},{9,17},{17,25},{25,1},{2,10},{10... | collective-permute-start | bytes 786440 | tf_op jit(solution)/shard_map/ppermute | solution.py:36
  97.3 3.7 %collective-permute-start.14 = (f32[64,256]{1,0:T(8,128)S(1)}, f32[64,256]{1,0:T(8,128)S(1)}, u32[]{:S(2)}, u32[]{:S(2)}) collective-permute-start(f32[64,256]{1,0:T(8,128)S(1)} %get-tuple-element.19), channel_id=1, source_target_pairs={{0,3},{1,0},{2,1},{3,2},{4,7},{5,4},{6,5},{7,6},{8,11},{9,8},{10,9... | collective-permute-start | bytes 196616 | tf_op jit(solution)/shard_map/ppermute | solution.py:36
  99.4 4.9 %collective-permute-start.13 = (f32[64,256]{1,0:T(8,128)S(1)}, f32[64,256]{1,0:T(8,128)S(1)}, u32[]{:S(2)}, u32[]{:S(2)}) collective-permute-start(f32[64,256]{1,0:T(8,128)S(1)} %get-tuple-element.20), channel_id=1, source_target_pairs={{0,2},{1,3},{2,0},{3,1},{4,6},{5,7},{6,4},{7,5},{8,10},{9,11},{10,... | collective-permute-start | bytes 196616 | tf_op jit(solution)/shard_map/ppermute | solution.py:36
  100.8 5.3 %collective-permute-start.12 = (f32[64,256]{1,0:T(8,128)S(1)}, f32[64,256]{1,0:T(8,128)S(1)}, u32[]{:S(2)}, u32[]{:S(2)}) collective-permute-start(f32[64,256]{1,0:T(8,128)S(1)} %get-tuple-element.18), channel_id=1, source_target_pairs={{0,1},{1,2},{2,3},{3,0},{4,5},{5,6},{6,7},{7,4},{8,9},{9,10},{10,1... | collective-permute-start | bytes 196616 | tf_op jit(solution)/shard_map/ppermute | solution.py:36
  106.5 4.1 %collective-permute-start.16 = (f32[16,256]{1,0:T(8,128)S(1)}, f32[16,256]{1,0:T(8,128)S(1)}, u32[]{:S(2)}, u32[]{:S(2)}) collective-permute-start(f32[16,256]{1,0:T(8,128)S(1)} %get-tuple-element.25), channel_id=1, source_target_pairs={{0,16},{8,24},{16,0},{24,8},{1,17},{9,25},{17,1},{25,9},{2,18},{10... | collective-permute-start | bytes 49160 | tf_op jit(solution)/shard_map/ppermute | solution.py:36
  107.7 3.8 %collective-permute-start.15 = (f32[16,256]{1,0:T(8,128)S(1)}, f32[16,256]{1,0:T(8,128)S(1)}, u32[]{:S(2)}, u32[]{:S(2)}) collective-permute-start(f32[16,256]{1,0:T(8,128)S(1)} %get-tuple-element.23), channel_id=1, source_target_pairs={{0,8},{8,16},{16,24},{24,0},{1,9},{9,17},{17,25},{25,1},{2,10},{10... | collective-permute-start | bytes 49160 | tf_op jit(solution)/shard_map/ppermute | solution.py:36
  111.5 2.7 %collective-permute-start.18 = (f32[16,256]{1,0:T(8,128)S(1)}, f32[16,256]{1,0:T(8,128)S(1)}, u32[]{:S(2)}, u32[]{:S(2)}) collective-permute-start(f32[16,256]{1,0:T(8,128)S(1)} %add_add_fusion.1), channel_id=1, source_target_pairs={{0,32},{32,0},{64,96},{96,64},{128,160},{160,128},{192,224},{224,1... | collective-permute-start | bytes 49160 | tf_op jit(solution)/shard_map/ppermute | solution.py:317
  114.2 3.5 %collective-permute-start.19 = (f32[16,256]{1,0:T(8,128)S(1)}, f32[16,256]{1,0:T(8,128)S(1)}, u32[]{:S(2)}, u32[]{:S(2)}) collective-permute-start(f32[16,256]{1,0:T(8,128)S(1)} %add.104), channel_id=1, source_target_pairs={{0,64},{32,96},{64,0},{96,32},{128,192},{160,224},{192,128},{224,1... | collective-permute-start | bytes 49160 | tf_op jit(solution)/shard_map/ppermute | solution.py:317
  117.7 3.8 %collective-permute-start.20 = (f32[16,256]{1,0:T(8,128)S(1)}, f32[16,256]{1,0:T(8,128)S(1)}, u32[]{:S(2)}, u32[]{:S(2)}) collective-permute-start(f32[16,256]{1,0:T(8,128)S(1)} %add.105), channel_id=1, source_target_pairs={{0,224},{32,192},{64,160},{96,128},{128,96},{160,64},{192,32},{224... | collective-permute-start | bytes 49160 | tf_op jit(solution)/shard_map/ppermute | solution.py:317
  122.3 11.3 %all-to-all-start.2 = ((f32[16,16,256]{2,1,0:T(8,128)}), f32[16,16,256]{2,1,0:T(8,128)S(1)}, u32[]{:S(2)}, u32[]{:S(2)}) async-start(f32[16,16,256]{2,1,0:T(8,128)} %broadcast_in_dim.27), calls=%async_computation.2 | async-start | bytes 524288 | tf_op jit(solution)/shard_map/all_to_all | solution.py:27
  133.6 37.3 %all-to-all-start.4 = ((bf16[256,8,128]{2,1,0:T(8,128)(2,1)}), bf16[256,8,128]{2,1,0:T(8,128)(2,1)S(1)}, u32[]{:S(2)}, u32[]{:S(2)}) async-start(bf16[256,8,128]{2,1,0:T(8,128)(2,1)} %bitcast.15), calls=%async_computation.4 | async-start | bytes 1048576 | tf_op jit(solution)/shard_map/all_to_all | solution.py:27
  150.9 3.4 %collective-permute-start.21 = (f32[256,256]{1,0:T(8,128)S(1)}, f32[256,256]{1,0:T(8,128)S(1)}, u32[]{:S(2)}, u32[]{:S(2)}) collective-permute-start(f32[256,256]{1,0:T(8,128)S(1)} %bitcast.43), channel_id=1, source_target_pairs={{0,4},{4,0},{1,5},{5,1},{2,6},{6,2},{3,7},{7,3},{8,12},{12,8},{9,1... | collective-permute-start | bytes 786440 | tf_op jit(solution)/shard_map/ppermute | solution.py:36
  (8 other events, 133.3 us)
